TPU v7x, 512 devices: a whole 4x8x8 slice. The times are simulated.
512 devices in a mesh: gx: 8 (over z), gy: 8 (over y), gz: 8 (over x, core).
Axes of the slice: x: 4, y: 8, z: 8, core: 2. Of those that a mesh axis runs over, the one named last changes fastest.
Arguments:
- strain: float32 [2, 4, 128, 128, 1024], P(None, None, 'gx', 'gy', 'gz'), may hold values from -6 to 6
- cell_shell_index: int32 [128, 128, 1024], P('gx', 'gy', 'gz'), may hold values from 0 to 255
- onset_step: int32 [256], replicated, may hold values from 0 to 1
Outputs:
- psi_four: float32 [2, 4, 128, 128, 1024], P(None, None, 'gx', 'gy', 'gz')
- energy: float32 [8, 4, 256], P('gx', None, ('gy', 'gz'))
All inputs are finite; a program needn't handle non-finite values.
Results may differ from a plain program's by a relative error of at most 0.00007.
Values sent between devices are 32-bit elements; how exact they have to be, the bound alone decides.
A program may use at most 64 MiB of HBM per device.

v0:
```python
import jax
import jax.numpy as jnp
from jax import lax
from jax.sharding import PartitionSpec as P

first_coef = ((-2, 1.0), (-1, -8.0), (1, 8.0), (2, -1.0))
second_coef = ((-2, -1.0), (-1, 16.0), (0, -30.0), (1, 16.0), (2, -1.0))


def extended(value, sides, width):
    edges = {}
    for axis, dim in sides:
        peers, length = (lax.axis_size(axis), value.shape[dim])
        up = [(i, (i + 1) % peers) for i in range(peers - 1)]
        last = lax.slice_in_dim(value, length - width, length, axis=dim)
        leading = lax.slice_in_dim(value, 0, width, axis=dim)
        edges[dim] = (
            lax.ppermute(last, axis, up),
            lax.ppermute(leading, axis, [(b, a) for a, b in up]),
        )
    done = []
    for _, dim in sides:
        low, high = edges[dim]
        around = [(width, width) if d in done else (0, 0) for d in range(value.ndim)]
        value = jnp.concatenate([jnp.pad(low, around), value, jnp.pad(high, around)], axis=dim)
        done.append(dim)
    return value


def extended_2(cells, sides, width):
    for axis, dim in sides:
        count = lax.axis_size(axis)
        ends = count - 1
        head = lax.slice_in_dim(cells, 0, width, axis=dim)
        tail = lax.slice_in_dim(cells, cells.shape[dim] - width, cells.shape[dim], axis=dim)
        cells = jnp.concatenate(
            [
                lax.ppermute(tail, axis, [(i, (i + 1) % count) for i in range(ends)]),
                cells,
                lax.ppermute(head, axis, [((i + 1) % count, i) for i in range(ends)]),
            ],
            axis=dim,
        )
    return cells


def split_up(value, dim, peers):
    lengths = value.shape
    blocks = value.reshape(*lengths[:dim], peers, lengths[dim] // peers, *lengths[dim + 1 :])
    return jnp.moveaxis(blocks, dim, 0)


def sent_and_summed(value, axis, dim):
    blocks = split_up(value, dim, lax.axis_size(axis))
    arrived = lax.all_to_all(blocks, axis, split_axis=0, concat_axis=0, tiled=True)
    return arrived.sum(axis=0)


def sent_to_all(value, axis):
    peers = lax.axis_size(axis)
    return lax.all_to_all(
        jnp.broadcast_to(value[None], (peers, *value.shape)), axis, 0, 0, tiled=True
    )


def folded_in_pairs(pieces, combine):
    while len(jax.tree.leaves(pieces)[0]) > 1:
        pieces = jax.vmap(combine)(*(pieces[side::2] for side in (0, 1)))
    return pieces[0]


def carried_in(value, axis, combine, identity):
    peers, here = (lax.axis_size(axis), lax.axis_index(axis))
    passed = jnp.arange(peers) < here

    def kept(part, zero, own):
        part = jnp.where(
            passed.reshape(-1, *(1 for _ in own.shape)), part, jnp.asarray(zero, own.dtype)
        )
        return part

    pieces = sent_to_all(value, axis)
    return folded_in_pairs(kept(pieces, identity, value), combine)


def along_z(padded, cells_z):
    views = {}
    for offset in (-2, -1, 0, 1, 2):
        views[offset] = padded[:, :, :, :, 2 + offset : 2 + offset + cells_z]
    first_z = sum((w * views[k] for k, w in first_coef)) / 12.0
    second_z = sum((w * views[k] for k, w in second_coef)) / 12.0
    return (views[0], first_z, second_z)


def body(strain, cell_shell_index, onset_step):
    cells_x, cells_y, cells_z = (strain.shape[2], strain.shape[3], strain.shape[4])
    steps_count = strain.shape[1]
    shell_count = onset_step.shape[0]
    padded = extended(strain, (("gx", 2), ("gy", 3), ("gz", 4)), 2)
    center, first_z, second_zfull = along_z(padded, cells_z)
    deriv_z = first_z[:, :, 2 : 2 + cells_x, 2 : 2 + cells_y, :]
    padded_y = extended_2(deriv_z, (("gy", 3),), 2)
    mixed_yz = (
        sum((w * padded_y[:, :, :, 2 + k : 2 + k + cells_y, :] for k, w in first_coef)) / 12.0
    )
    second_x = (
        sum((w * center[:, :, 2 + k : 2 + k + cells_x, 2 : 2 + cells_y, :] for k, w in second_coef))
        / 12.0
    )
    second_y = (
        sum((w * center[:, :, 2 : 2 + cells_x, 2 + k : 2 + k + cells_y, :] for k, w in second_coef))
        / 12.0
    )
    second_z = second_zfull[:, :, 2 : 2 + cells_x, 2 : 2 + cells_y, :]
    combo = second_x + second_y - second_z
    real_part = 0.5 * combo[0] - mixed_yz[1]
    imag_part = -0.5 * combo[1] - mixed_yz[0]
    psi_four = jnp.stack([real_part, imag_part])
    bondi_news = jnp.cumsum(psi_four, axis=1) * 0.25
    total_x = cells_x * lax.axis_size("gx")
    total_y = cells_y * lax.axis_size("gy")
    total_z = cells_z * lax.axis_size("gz")
    start_x = (lax.axis_index("gx") * cells_x).astype(jnp.float32)
    start_y = (lax.axis_index("gy") * cells_y).astype(jnp.float32)
    start_z = (lax.axis_index("gz") * cells_z).astype(jnp.float32)
    position_along_x = (jnp.arange(cells_x, dtype=jnp.float32) + start_x + 0.5) / total_x - 0.5
    position_along_y = (jnp.arange(cells_y, dtype=jnp.float32) + start_y + 0.5) / total_y - 0.5
    position_along_z = (jnp.arange(cells_z, dtype=jnp.float32) + start_z + 0.5) / total_z - 0.5
    radius_squared = (
        position_along_x[:, None, None] ** 2
        + position_along_y[None, :, None] ** 2
        + position_along_z[None, None, :] ** 2
        + 0.05
    )
    energy_flux = radius_squared[None] * (bondi_news[0] ** 2 + bondi_news[1] ** 2)
    plane_len = cells_y * cells_z
    flux_planes = energy_flux.reshape(steps_count, cells_x, plane_len)
    shell_planes = cell_shell_index.reshape(cells_x, plane_len)
    shell_labels = jnp.arange(shell_count, dtype=jnp.int32)

    def bin_plane(total, pieces):
        shell_piece, plane = pieces
        flux_piece = lax.dynamic_index_in_dim(flux_planes, plane, 1, keepdims=False)
        one_hot = (shell_piece[:, None] == shell_labels[None, :]).astype(jnp.float32)
        return (total + jnp.dot(flux_piece, one_hot, precision=lax.Precision.HIGHEST), None)

    binned, unused = lax.scan(
        bin_plane,
        jnp.zeros((steps_count, shell_count), jnp.float32),
        (shell_planes, jnp.arange(cells_x, dtype=jnp.int32)),
    )
    live = (jnp.arange(steps_count, dtype=jnp.int32)[:, None] >= onset_step[None, :]).astype(
        jnp.float32
    )
    scale = 0.25 * shell_count / (total_x * total_y * total_z)
    partial_value = jnp.cumsum(binned * live, axis=0) * scale

    def add_terms(earlier, later):
        return earlier + later

    reduced = sent_and_summed(partial_value, ("gy", "gz"), 1)
    before = carried_in(reduced, "gx", add_terms, jnp.zeros_like(reduced))
    energy = (before + reduced)[None]
    return (psi_four, energy)


def solution(mesh):
    placed = (P(None, None, "gx", "gy", "gz"), P("gx", "gy", "gz"), P())
    return jax.shard_map(
        body,
        mesh=mesh,
        in_specs=placed,
        out_specs=(P(None, None, "gx", "gy", "gz"), P("gx", None, ("gy", "gz"))),
        check_vma=False,
    )
```

profile of v0, /device:TPU:1, one launch (start us, length us, event | category | flops | bytes accessed | tf_op | source)
XLA Modules:
  0.0 172.6 jit_solution(8097845562536302447)
XLA Ops:
  0.6 1.8 %fusion.50 = (f32[2,4,2,16,128]{4,3,2,1,0:T(8,128)}, f32[2,4,2,16,128]{4,3,2,1,0:T(8,128)}) fusion(f32[2,4,16,16,128]{4,3,2,1,0:T(8,128)} %param.5), kind=kLoop, calls=%fused_computation.109 | loop fusion | bytes 524288 | tf_op jit(solution)/shard_map/slice | solution.py:16
  2.4 5.5 %collective-permute-start = (f32[2,4,2,16,128]{4,3,2,1,0:T(8,128)}, f32[2,4,2,16,128]{4,3,2,1,0:T(8,128)}, u32[]{:S(2)}, u32[]{:S(2)}) collective-permute-start(f32[2,4,2,16,128]{4,3,2,1,0:T(8,128)} %get-tuple-element.84), channel_id=1, source_target_pairs={{0,64},{64,128},{128,192},{192,256},{256,320},{320,384},{384,448},... | collective-permute-start | bytes 393224 | tf_op jit(solution)/shard_map/ppermute | solution.py:18
  7.9 2.0 %fusion.49 = (f32[2,4,16,2,128]{4,3,2,1,0:T(2,128)}, f32[2,4,16,2,128]{4,3,2,1,0:T(2,128)}) fusion(f32[2,4,16,16,128]{4,3,2,1,0:T(8,128)} %param.5), kind=kLoop, calls=%fused_computation.108 | loop fusion | bytes 524288 | tf_op jit(solution)/shard_map/slice | solution.py:15
  9.9 3.8 %collective-permute-start.2 = (f32[2,4,16,2,128]{4,3,2,1,0:T(2,128)}, f32[2,4,16,2,128]{4,3,2,1,0:T(2,128)}, u32[]{:S(2)}, u32[]{:S(2)}) collective-permute-start(f32[2,4,16,2,128]{4,3,2,1,0:T(2,128)} %get-tuple-element.81), channel_id=1, source_target_pairs={{0,8},{8,16},{16,24},{24,32},{32,40},{40,48},{48,56},{1,9},{9,17},... | collective-permute-start | bytes 393224 | tf_op jit(solution)/shard_map/ppermute | solution.py:18
  13.7 1.3 collective-permute-start.3
  15.4 0.8 copy.11
  16.2 4.2 %collective-permute-start.4 = (f32[2,4,16,16,2]{3,2,4,1,0:T(8,128)S(1)}, f32[2,4,16,16,2]{3,2,4,1,0:T(8,128)S(1)}, u32[]{:S(2)}, u32[]{:S(2)}) collective-permute-start(f32[2,4,16,16,2]{3,2,4,1,0:T(8,128)S(1)} %copy.11), channel_id=1, source_target_pairs={{0,1},{1,2},{2,3},{3,4},{4,5},{5,6},{6,7},{8,9},{9,10},{10,11},{11... | collective-permute-start | bytes 49160 | tf_op jit(solution)/shard_map/ppermute | solution.py:18
  20.5 0.8 copy.12
  21.3 1.9 %collective-permute-start.5 = (f32[2,4,16,16,2]{3,2,4,1,0:T(8,128)S(1)}, f32[2,4,16,16,2]{3,2,4,1,0:T(8,128)S(1)}, u32[]{:S(2)}, u32[]{:S(2)}) collective-permute-start(f32[2,4,16,16,2]{3,2,4,1,0:T(8,128)S(1)} %copy.12), channel_id=1, source_target_pairs={{1,0},{2,1},{3,2},{4,3},{5,4},{6,5},{7,6},{9,8},{10,9},{11,10},{12... | collective-permute-start | bytes 49160 | tf_op jit(solution)/shard_map/ppermute | solution.py:19
  23.5 0.7 copy.23
  24.2 1.3 collective-permute-start.1
  25.5 0.8 copy.13
  26.3 1.6 collective-permute-done.5
  28.0 1.8 %copy.14 = f32[2,4,16,16,2]{4,3,2,1,0:T(8,128)} copy(f32[2,4,16,16,2]{3,2,4,1,0:T(8,128)S(1)} %collective-permute-done.5) | data formatting | bytes 32768
  29.8 1.0 pad.14
  30.8 1.0 constant_dynamic-update-slice_fusion.1
  31.8 1.0 pad.15
  33.0 1.0 constant_dynamic-update-slice_fusion.2
  34.1 3.9 %select_maximum_fusion.1 = (f32[2,4,20,20,130]{4,3,2,1,0:T(8,128)S(1)}, f32[2,4,20,20,130]{4,3,2,1,0:T(8,128)}) fusion(f32[2,4,16,16,2]{4,3,2,1,0:T(8,128)S(1)} %copy.13, f32[2,4,20,2,128]{4,3,2,1,0:T(2,128)S(1)} %pad.15, f32[2,4,20,16,128]{4,3,2,1,0:T(8,128)S(1)} %get-tuple-element.88, f32[2,4,20,2,128]{4,3,2,1,0:T(2,128)S(1)} %pad.14, ...), kind=kLoop, calls=%fused_computation.11 | loop fusion | flops 4160000 | bytes 4999168 | tf_op jit(solution)/shard_map/concatenate | solution.py:25
  37.9 8.7 %fusion.46 = (f32[2,4,20,20,128]{4,3,2,1,0:T(8,128)}, f32[2,4,20,20,128]{4,3,2,1,0:T(8,128)}, f32[2,4,20,20,128]{4,3,2,1,0:T(8,128)}, f32[2,4,20,20,128]{4,3,2,1,0:T(8,128)}, f32[2,4,20,20,128]{4,3,2,1,0:T(8,128)}) fusion(f32[2,4,20,20,130]{4,3,2,1,0:T(8,128)S(1)} %get-tuple-element.74, f32[2,4,20,20,130]{4,3,2,1,0:T(8,128)} %get-tuple-element.75), kind=kLoop, calls=%fused_computation.105 | loop fusion | flops 2867200 | bytes 14745600 | tf_op jit(solution)/shard_map/slice | solution.py:89
  46.7 1.3 fusion.47
  48.0 4.3 %collective-permute-start.6 = (f32[2,4,16,2,128]{4,3,2,1,0:T(2,128)S(1)}, f32[2,4,16,2,128]{4,3,2,1,0:T(2,128)S(1)}, u32[]{:S(2)}, u32[]{:S(2)}) collective-permute-start(f32[2,4,16,2,128]{4,3,2,1,0:T(2,128)S(1)} %get-tuple-element.72), channel_id=1, source_target_pairs={{0,8},{8,16},{16,24},{24,32},{32,40},{40,48},{48,56},{1,9},{9,17},... | collective-permute-start | bytes 393224 | tf_op jit(solution)/shard_map/ppermute | solution.py:38
  52.3 1.3 collective-permute-start.7
  53.6 4.0 %fusion.22 = f32[2,4,16,16,128]{4,3,2,1,0:T(8,128)S(1)} fusion(f32[2,4,20,2,128]{4,3,2,1,0:T(2,128)S(1)} %copy-done.5, f32[2,4,20,16,128]{4,3,2,1,0:T(8,128)S(1)} %get-tuple-element.88, f32[2,4,20,2,128]{4,3,2,1,0:T(2,128)S(1)} %copy-done.7, f32[2,4,20,20,128]{4,3,2,1,0:T(8,128)} %get-tuple-element.68, f32[2,4,20,20,128]{4,3,2,1,0:T(8,128)} %get-tuple-element.67, ...), kind=kLoop, calls=%fused_computation.42 | loop fusion | flops 9175040 | bytes 12124160 | tf_op jit(solution)/shard_map/sub | solution.py:115
  58.0 0.7 fusion.12
  59.0 3.7 %reduce-window_multiply_fusion = f32[2,4,16,16,128]{4,3,2,1,0:T(8,128)S(1)} fusion(f32[2,4,16,16,128]{4,3,2,1,0:T(8,128)S(1)} %pad_maximum_fusion.4), kind=kOutput, calls=%fused_computation.25 | output fusion | flops 1048576 | bytes 2097152 | tf_op jit(solution)/shard_map/jit(cumsum)/reduce_window_sum | solution.py:119
  62.9 67.5 %while.11 = (s32[]{:T(128)}, f32[4,256]{1,0:T(4,128)S(1)}, s32[16]{0:T(128)S(1)}, f32[4,16,2048]{2,1,0:T(8,128)S(1)}, s32[16,2048]{1,0:T(8,128)}, /*index=5*/s32[]{:T(128)}, s32[]{:T(128)}, s32[]{:T(128)}) while((s32[]{:T(128)}, f32[4,256]{1,0:T(4,128)S(1)}, s32[16]{0:T(128)S(1)}, f32[4,16,2048]{2,1,0:T(8,128)S(1)}, ...), condition=%wide.region_2.3_spmd.clone, body=%wide.region_1.2_spmd.clone.sunk | while | flops 25692164 | bytes 131221 | solution.py:147
  65.5 0.9 constant_dynamic-slice_fusion.4
  66.3 0.8 fusion.56
  67.1 0.7 dynamic_slice.22
  69.7 0.9 constant_dynamic-slice_fusion.4
  70.5 0.8 fusion.56
  71.3 0.7 dynamic_slice.22
  73.9 0.9 constant_dynamic-slice_fusion.4
  74.8 0.8 fusion.56
  78.1 0.9 constant_dynamic-slice_fusion.4
  79.0 0.8 fusion.56
  82.4 0.9 constant_dynamic-slice_fusion.4
  83.2 0.8 fusion.56
  86.6 0.9 constant_dynamic-slice_fusion.4
  87.4 0.8 fusion.56
  90.8 0.9 constant_dynamic-slice_fusion.4
  91.7 0.8 fusion.56
  95.0 0.9 constant_dynamic-slice_fusion.4
  95.9 0.8 fusion.56
  99.2 0.9 constant_dynamic-slice_fusion.4
  100.1 0.8 fusion.56
  103.5 0.9 constant_dynamic-slice_fusion.4
  104.3 0.8 fusion.56
  107.7 0.9 constant_dynamic-slice_fusion.4
  108.5 0.8 fusion.56
  111.9 0.9 constant_dynamic-slice_fusion.4
  112.8 0.8 fusion.56
  116.1 0.9 constant_dynamic-slice_fusion.4
  117.0 0.8 fusion.56
  120.3 0.9 constant_dynamic-slice_fusion.4
  121.2 0.8 fusion.56
  124.6 0.9 constant_dynamic-slice_fusion.4
  125.4 0.8 fusion.56
  128.8 0.9 constant_dynamic-slice_fusion.4
  129.6 0.8 fusion.56
  130.8 23.2 %all_to_all.10 = f32[64,4,4]{2,1,0:T(4,128)S(1)} all-to-all(f32[64,4,4]{2,1,0:T(4,128)S(1)} %copy.9), channel_id=1, replica_groups=mesh['gx'=8,'gy'=8,'gz'=8] {'gy','gz'}, dimensions={0} | all-to-all | bytes 8192 | tf_op jit(solution)/shard_map/all_to_all | solution.py:55
  154.7 10.6 %all-to-all-start.1 = ((f32[8,4,4]{2,1,0:T(4,128)}), f32[8,4,4]{2,1,0:T(4,128)S(1)}, u32[]{:S(2)}, u32[]{:S(2)}) async-start(f32[8,4,4]{2,1,0:T(4,128)} %broadcast_in_dim.16), calls=%async_computation.1 | async-start | bytes 32768 | tf_op jit(solution)/shard_map/all_to_all | solution.py:61
  165.3 6.6 %all-to-all-done.1 = f32[8,4,4]{2,1,0:T(4,128)S(1)} async-done(((f32[8,4,4]{2,1,0:T(4,128)}), f32[8,4,4]{2,1,0:T(4,128)S(1)}, u32[]{:S(2)}, u32[]{:S(2)}) %all-to-all-start.1) | async-done | bytes 544 | tf_op jit(solution)/shard_map/all_to_all | solution.py:61
  (84 shorter events, 13.0 us)
Async XLA Ops:
  0.6 14.4 %copy-start = (f32[2,4,16,16,128]{4,3,2,1,0:T(8,128)S(1)}, f32[2,4,16,16,128]{4,3,2,1,0:T(8,128)}, u32[]{:S(2)}) copy-start(f32[2,4,16,16,128]{4,3,2,1,0:T(8,128)} %param.5) | copy-start | bytes 3145732
  2.4 28.3 %collective-permute-start = (f32[2,4,2,16,128]{4,3,2,1,0:T(8,128)}, f32[2,4,2,16,128]{4,3,2,1,0:T(8,128)}, u32[]{:S(2)}, u32[]{:S(2)}) collective-permute-start(f32[2,4,2,16,128]{4,3,2,1,0:T(8,128)} %get-tuple-element.84), channel_id=1, source_target_pairs={{0,64},{64,128},{128,192},{192,256},{256,320},{320,384},{384,448},... | collective-permute-start | bytes 393224 | tf_op jit(solution)/shard_map/ppermute | solution.py:18
  9.9 19.9 %collective-permute-start.2 = (f32[2,4,16,2,128]{4,3,2,1,0:T(2,128)}, f32[2,4,16,2,128]{4,3,2,1,0:T(2,128)}, u32[]{:S(2)}, u32[]{:S(2)}) collective-permute-start(f32[2,4,16,2,128]{4,3,2,1,0:T(2,128)} %get-tuple-element.81), channel_id=1, source_target_pairs={{0,8},{8,16},{16,24},{24,32},{32,40},{40,48},{48,56},{1,9},{9,17},... | collective-permute-start | bytes 393224 | tf_op jit(solution)/shard_map/ppermute | solution.py:18
  13.7 18.0 %collective-permute-start.3 = (f32[2,4,16,2,128]{4,3,2,1,0:T(2,128)}, f32[2,4,16,2,128]{4,3,2,1,0:T(2,128)}, u32[]{:S(2)}, u32[]{:S(2)}) collective-permute-start(f32[2,4,16,2,128]{4,3,2,1,0:T(2,128)} %get-tuple-element.82), channel_id=1, source_target_pairs={{8,0},{16,8},{24,16},{32,24},{40,32},{48,40},{56,48},{9,1},{17,9},... | collective-permute-start | bytes 393224 | tf_op jit(solution)/shard_map/ppermute | solution.py:19
  15.4 8.1 %copy-start.8 = (s32[16,16,128]{2,1,0:T(8,128)S(1)}, s32[16,16,128]{2,1,0:T(8,128)}, u32[]{:S(2)}) copy-start(s32[16,16,128]{2,1,0:T(8,128)} %param.6) | copy-start | bytes 393220
  16.2 8.0 %collective-permute-start.4 = (f32[2,4,16,16,2]{3,2,4,1,0:T(8,128)S(1)}, f32[2,4,16,16,2]{3,2,4,1,0:T(8,128)S(1)}, u32[]{:S(2)}, u32[]{:S(2)}) collective-permute-start(f32[2,4,16,16,2]{3,2,4,1,0:T(8,128)S(1)} %copy.11), channel_id=1, source_target_pairs={{0,1},{1,2},{2,3},{3,4},{4,5},{5,6},{6,7},{8,9},{9,10},{10,11},{11... | collective-permute-start | bytes 49160 | tf_op jit(solution)/shard_map/ppermute | solution.py:18
  21.3 6.7 %collective-permute-start.5 = (f32[2,4,16,16,2]{3,2,4,1,0:T(8,128)S(1)}, f32[2,4,16,16,2]{3,2,4,1,0:T(8,128)S(1)}, u32[]{:S(2)}, u32[]{:S(2)}) collective-permute-start(f32[2,4,16,16,2]{3,2,4,1,0:T(8,128)S(1)} %copy.12), channel_id=1, source_target_pairs={{1,0},{2,1},{3,2},{4,3},{5,4},{6,5},{7,6},{9,8},{10,9},{11,10},{12... | collective-permute-start | bytes 49160 | tf_op jit(solution)/shard_map/ppermute | solution.py:19
  24.2 8.8 %collective-permute-start.1 = (f32[2,4,2,16,128]{4,3,2,1,0:T(8,128)}, f32[2,4,2,16,128]{4,3,2,1,0:T(8,128)}, u32[]{:S(2)}, u32[]{:S(2)}) collective-permute-start(f32[2,4,2,16,128]{4,3,2,1,0:T(8,128)} %get-tuple-element.83), channel_id=1, source_target_pairs={{64,0},{128,64},{192,128},{256,192},{320,256},{384,320},{448,384},... | collective-permute-start | bytes 393224 | tf_op jit(solution)/shard_map/ppermute | solution.py:19
  30.7 3.3 %copy-start.4 = (f32[2,4,20,2,128]{4,3,2,1,0:T(2,128)}, f32[2,4,20,2,128]{4,3,2,1,0:T(2,128)S(1)}, u32[]{:S(2)}) copy-start(f32[2,4,20,2,128]{4,3,2,1,0:T(2,128)S(1)} %pad.14) | copy-start | bytes 491524
  32.7 1.3 copy-start.6
  32.7 1.3 copy-start.3
  37.9 15.7 %copy-start.5 = (f32[2,4,20,2,128]{4,3,2,1,0:T(2,128)S(1)}, f32[2,4,20,2,128]{4,3,2,1,0:T(2,128)}, u32[]{:S(2)}) copy-start(f32[2,4,20,2,128]{4,3,2,1,0:T(2,128)} %copy-done.4) | copy-start | bytes 491524
  37.9 15.7 %copy-start.7 = (f32[2,4,20,2,128]{4,3,2,1,0:T(2,128)S(1)}, f32[2,4,20,2,128]{4,3,2,1,0:T(2,128)}, u32[]{:S(2)}) copy-start(f32[2,4,20,2,128]{4,3,2,1,0:T(2,128)} %copy-done.6) | copy-start | bytes 491524
  48.0 9.8 %collective-permute-start.6 = (f32[2,4,16,2,128]{4,3,2,1,0:T(2,128)S(1)}, f32[2,4,16,2,128]{4,3,2,1,0:T(2,128)S(1)}, u32[]{:S(2)}, u32[]{:S(2)}) collective-permute-start(f32[2,4,16,2,128]{4,3,2,1,0:T(2,128)S(1)} %get-tuple-element.72), channel_id=1, source_target_pairs={{0,8},{8,16},{16,24},{24,32},{32,40},{40,48},{48,56},{1,9},{9,17},... | collective-permute-start | bytes 393224 | tf_op jit(solution)/shard_map/ppermute | solution.py:38
  52.3 5.7 %collective-permute-start.7 = (f32[2,4,16,2,128]{4,3,2,1,0:T(2,128)S(1)}, f32[2,4,16,2,128]{4,3,2,1,0:T(2,128)S(1)}, u32[]{:S(2)}, u32[]{:S(2)}) collective-permute-start(f32[2,4,16,2,128]{4,3,2,1,0:T(2,128)S(1)} %get-tuple-element.73), channel_id=1, source_target_pairs={{8,0},{16,8},{24,16},{32,24},{40,32},{48,40},{56,48},{9,1},{17,9},... | collective-permute-start | bytes 393224 | tf_op jit(solution)/shard_map/ppermute | solution.py:40
  53.6 4.0 %copy-start.1 = (f32[2,4,20,20,128]{4,3,2,1,0:T(8,128)S(1)}, f32[2,4,20,20,128]{4,3,2,1,0:T(8,128)}, u32[]{:S(2)}) copy-start(f32[2,4,20,20,128]{4,3,2,1,0:T(8,128)} %get-tuple-element.66) | copy-start | bytes 4915204
  58.9 3.9 %copy-start.2 = (f32[2,4,16,16,128]{4,3,2,1,0:T(8,128)}, f32[2,4,16,16,128]{4,3,2,1,0:T(8,128)S(1)}, u32[]{:S(2)}) copy-start(f32[2,4,16,16,128]{4,3,2,1,0:T(8,128)S(1)} %pad_maximum_fusion.4) | copy-start | bytes 3145732
  62.9 67.6 %copy-start.9 = (s32[256]{0:T(256)S(1)}, s32[256]{0:T(256)}, u32[]{:S(2)}) copy-start(s32[256]{0:T(256)} %param.7) | copy-start | bytes 3076
  154.7 17.2 %all-to-all-start.1 = ((f32[8,4,4]{2,1,0:T(4,128)}), f32[8,4,4]{2,1,0:T(4,128)S(1)}, u32[]{:S(2)}, u32[]{:S(2)}) async-start(f32[8,4,4]{2,1,0:T(4,128)} %broadcast_in_dim.16), calls=%async_computation.1 | async-start | bytes 32768 | tf_op jit(solution)/shard_map/all_to_all | solution.py:61
where the time goes:
time: 174 us; the launch traced here: 173 us
  local copies, waits for them, and re-layouts  40.3 us (23%)
  starting transfers between devices  34.2 us (20%)
  loops' own time  30.1 us (17%)
  blocking collectives  23.2 us (13%)
  other arithmetic  22.4 us (13%)
  matrix products  12.8 us (7%)
  waiting for transfers between devices  8.51 us (5%)
    another operation x1, loops' own time, body(): lax.scan(bin_plane, jnp.zeros((steps_count, shell_count), jnp.float32), (...  30.1 us
    dynamic_slice x32, local copies, waits for them, and re-layouts, body(): lax.scan(bin_plane, jnp.zeros((steps_count, shell_count), jnp.float32), (...  24.1 us
    all_to_all x1, blocking collectives, sent_and_summed(): lax.all_to_all(blocks, axis, split_axis=0, concat_axis=0, tiled=True)  23.2 us
    ppermute x3, starting transfers between devices, extended(): lax.ppermute(last, axis, up)  13.6 us
    dot_general x16, matrix products, bin_plane(): jnp.dot(flux_piece, one_hot, precision=lax.Precision.HIGHEST)  12.8 us
    all_to_all x1, starting transfers between devices, sent_to_all(): lax.all_to_all(jnp.broadcast_to(value[None], (peers, *value.shape)), axis...  10.6 us
    slice x1, other arithmetic, along_z(): views[offset] = padded[:, :, :, :, 2 + offset:2 + offset + cells_z]  8.74 us
    all_to_all x1, waiting for transfers between devices, sent_to_all(): lax.all_to_all(jnp.broadcast_to(value[None], (peers, *value.shape)), axis...  6.62 us
  transfers between devices with their start and end apart: 9, of which 3 were waited for; matrix products, arithmetic and copies ran while one was open for 9% of the time, Pallas kernels for 0%

commit v1 on v0

v1 whole, which is shorter than its diff:
```python
import jax
import jax.numpy as jnp
from jax import lax
from jax.experimental import pallas as pl
from jax.experimental.pallas import tpu as pltpu
from jax.sharding import PartitionSpec as P

MESH = pl.DeviceIdType.MESH
F32 = jnp.float32


def kernel(
    sizes,
    strain,
    shells,
    onset,
    psi_out,
    energy_out,
    field,
    shell,
    onsets,
    zpack,
    zlow,
    zhigh,
    firsts,
    seconds,
    psi,
    binned,
    parts,
    got_y,
    got_z,
    got_x,
    total_yz,
    in_sem,
    out_sem,
    halo_send,
    halo_recv,
    sum_send,
    sum_recv,
):
    nx, ny, nz = sizes
    gx, gy, gz = (lax.axis_index(a) for a in ("gx", "gy", "gz"))
    cx = 16
    ct = 8

    loads = [
        pltpu.make_async_copy(strain.at[c], field.at[2:18, 2:18, c], in_sem.at[c]) for c in range(ct)
    ]
    loads.append(pltpu.make_async_copy(shells, shell, in_sem.at[ct]))
    loads.append(pltpu.make_async_copy(onset, onsets, in_sem.at[ct + 1]))
    for load in loads:
        load.start()

    below = {"gx": gx > 0, "gy": gy > 0, "gz": gz > 0}
    above = {"gx": gx < nx - 1, "gy": gy < ny - 1, "gz": gz < nz - 1}
    at = {"gx": gx, "gy": gy, "gz": gz}
    count = {"gx": nx, "gy": ny, "gz": nz}

    barrier = pltpu.get_barrier_semaphore()
    for axis in ("gx", "gy", "gz"):
        for d in range(1, count[axis]):
            pl.semaphore_signal(
                barrier,
                inc=1,
                device_id={axis: lax.rem(at[axis] + d, count[axis])},
                device_id_type=MESH,
            )
    corners = []
    for has_y, step_y in ((below["gy"], -1), (above["gy"], 1)):
        for has_z, step_z in ((below["gz"], -1), (above["gz"], 1)):
            both = jnp.logical_and(has_y, has_z)
            corners.append((both, {"gy": gy + step_y, "gz": gz + step_z}))
    for both, peer in corners:

        @pl.when(both)
        def _(peer=peer):
            pl.semaphore_signal(barrier, inc=1, device_id=peer, device_id_type=MESH)

    greeted = nx - 1 + ny - 1 + nz - 1
    for both, _ in corners:
        greeted = greeted + both.astype(jnp.int32)

    def zero(where, ref):
        @pl.when(where)
        def _():
            ref[...] = jnp.zeros(ref.shape, F32)

    no = jnp.logical_not
    zero(no(below["gx"]), field.at[0:2, 2:18])
    zero(no(above["gx"]), field.at[18:20, 2:18])
    zero(no(below["gy"]), field.at[2:18, 0:2])
    zero(no(above["gy"]), field.at[2:18, 18:20])
    zero(no(below["gz"]), zlow.at[1:9])
    zero(no(above["gz"]), zhigh.at[1:9])
    zero(no(corners[0][0]), zlow.at[0])
    zero(no(corners[1][0]), zhigh.at[0])
    zero(no(corners[2][0]), zlow.at[9])
    zero(no(corners[3][0]), zhigh.at[9])

    lane = lax.broadcasted_iota(jnp.int32, (8, 128), 1)
    sub = lax.broadcasted_iota(jnp.int32, (8, 128), 0)
    slot_of = ((lane + 2) & 127) >> 2

    for load in loads:
        load.wait()

    def pack(x, acc):
        acc = list(acc)
        for b in range(8):
            for p in range(2):
                slot = 2 * x + p
                moved = pltpu.roll(field[x + 2, 2 * b + p + 2], 4 * slot, 1)
                acc[b] = jnp.where(slot_of == slot, moved, acc[b])
        return tuple(acc)

    packed = lax.fori_loop(0, cx, pack, tuple(jnp.zeros((8, 128), F32) for _ in range(8)))
    for b in range(8):
        zpack[b] = packed[b]

    pl.semaphore_wait(barrier, greeted)

    def halo(i, has, src, dst, peer, sends):
        copy = pltpu.make_async_remote_copy(
            src_ref=src,
            dst_ref=dst,
            send_sem=halo_send.at[i],
            recv_sem=halo_recv.at[i],
            device_id=peer,
            device_id_type=MESH,
        )
        sends.append((has, copy))

    sends = []
    halo(0, above["gz"], zpack, zlow.at[1:9], {"gz": gz + 1}, sends)
    halo(1, below["gz"], zpack, zhigh.at[1:9], {"gz": gz - 1}, sends)
    halo(2, corners[3][0], zpack.at[7], zlow.at[0], corners[3][1], sends)
    halo(3, corners[2][0], zpack.at[7], zhigh.at[0], corners[2][1], sends)
    halo(4, corners[1][0], zpack.at[0], zlow.at[9], corners[1][1], sends)
    halo(5, corners[0][0], zpack.at[0], zhigh.at[9], corners[0][1], sends)
    halo(6, above["gy"], field.at[2:18, 16:18], field.at[2:18, 0:2], {"gy": gy + 1}, sends)
    halo(7, below["gy"], field.at[2:18, 2:4], field.at[2:18, 18:20], {"gy": gy - 1}, sends)
    halo(8, above["gx"], field.at[16:18, 2:18], field.at[0:2, 2:18], {"gx": gx + 1}, sends)
    halo(9, below["gx"], field.at[2:4, 2:18], field.at[18:20, 2:18], {"gx": gx - 1}, sends)
    arrives = [
        below["gz"],
        above["gz"],
        corners[0][0],
        corners[1][0],
        corners[2][0],
        corners[3][0],
        below["gy"],
        above["gy"],
        below["gx"],
        above["gx"],
    ]
    for has, copy in sends:

        @pl.when(has)
        def _(copy=copy):
            copy.start()

    def arrive(i):
        @pl.when(arrives[i])
        def _():
            sends[i][1].wait_recv()

    for i in range(6):
        arrive(i)

    def along_z(ys):
        edges = {b: jnp.where((lane & 2) != 0, zlow[b], zhigh[b]) for b in sorted({y // 2 for y in ys})}

        def step(x, _):
            for y in ys:
                f = field[x + 2, y]
                end = pltpu.roll(edges[y // 2], 128 - 4 * (2 * x + y % 2), 1)
                up1 = pltpu.roll(jnp.where(lane >= 1, f, end), 127, 1)
                up2 = pltpu.roll(jnp.where(lane >= 2, f, end), 126, 1)
                down1 = pltpu.roll(jnp.where(lane < 127, f, end), 1, 1)
                down2 = pltpu.roll(jnp.where(lane < 126, f, end), 2, 1)
                firsts[x, y] = 8.0 * (up1 - down1) - (up2 - down2)
                if 2 <= y < 18:
                    seconds[x, y - 2] = 16.0 * (up1 + down1) - (up2 + down2)
            return 0

        lax.fori_loop(0, cx, step, 0)

    along_z(list(range(2, 18)))
    for i in range(6, 10):
        arrive(i)
    along_z([0, 1, 18, 19])

    signs = jnp.where(sub < 4, 1.0 / 24.0, -1.0 / 24.0).astype(F32)
    step_of = sub & 3
    uz = (lane + gz * 128).astype(F32)
    uz = (uz + 0.5) / (nz * 128) - 0.5
    uz2 = uz * uz + 0.05

    def main(x, total):
        ux = (x + gx * cx).astype(F32)
        ux = (ux + 0.5) / (nx * cx) - 0.5
        ux2 = uz2 + ux * ux
        lefts, rights = [], []
        for y in range(16):
            f = field[x + 2, y + 2]
            near = (field[x + 1, y + 2] + field[x + 3, y + 2]) + (field[x + 2, y + 1] + field[x + 2, y + 3])
            far = (field[x, y + 2] + field[x + 4, y + 2]) + (field[x + 2, y] + field[x + 2, y + 4])
            combo = (16.0 * near - far) - (seconds[x, y] + 30.0 * f)
            mixed = 8.0 * (firsts[x, y + 3] - firsts[x, y + 1]) - (firsts[x, y + 4] - firsts[x, y])
            value = combo * signs - pltpu.roll(mixed, 4, 0) * (1.0 / 144.0)
            psi[x, y] = value
            news = value + jnp.where(step_of >= 1, pltpu.roll(value, 1, 0), 0.0)
            news = news + jnp.where(step_of >= 2, pltpu.roll(news, 2, 0), 0.0)
            power = news * news
            power = power + pltpu.roll(power, 4, 0)
            uy = (gy * 16 + y).astype(F32)
            uy = (uy + 0.5) / (ny * 16) - 0.5
            flux = power * ((ux2 + uy * uy) * 0.0625)
            high = flux.astype(jnp.bfloat16).astype(F32)
            split = jnp.where(sub < 4, high, flux - high)
            label = jnp.broadcast_to(shell[x, pl.ds(y, 1), :], (8, 128))
            outer = label >> 5
            inner = label & 31
            lefts.append(jnp.concatenate([jnp.where(outer == k, split, 0.0) for k in range(8)], axis=0))
            rights.append(
                jnp.concatenate([jnp.where(inner == sub + 8 * j, 1.0, 0.0).astype(F32) for j in range(4)], axis=0)
            )
        left = jnp.concatenate(lefts, axis=1)
        right = jnp.concatenate(rights, axis=1)
        return total + lax.dot_general(
            left, right, (((1,), (1,)), ((), ())), preferred_element_type=F32
        )

    total = lax.fori_loop(0, cx, main, jnp.zeros((64, 32), F32))

    stores = [
        pltpu.make_async_copy(psi.at[:, :, c], psi_out.at[c], out_sem.at[c]) for c in range(ct)
    ]
    for store in stores:
        store.start()

    def by_step(x, moves):
        moved = x
        for t in range(1, 4):
            moved = jnp.where(step_of == t, pltpu.roll(x, moves[t], 1), moved)
        return moved

    binned[...] = jnp.zeros((64, 128), F32)
    binned[:, 0:32] = total
    for k in range(8):
        spread = by_step(binned[8 * k : 8 * k + 8, :], (0, 32, 64, 96))
        parts[k] = jnp.sum(spread, axis=0, keepdims=True)

    def exchange(axis, base, src, dst, use):
        me, n = at[axis], count[axis]
        copies = []
        for d in range(1, n):
            peer = lax.rem(me + d, n)
            copies.append(
                pltpu.make_async_remote_copy(
                    src_ref=src(peer),
                    dst_ref=dst.at[d],
                    send_sem=sum_send.at[base + d],
                    recv_sem=sum_recv.at[base + d],
                    device_id={axis: peer},
                    device_id_type=MESH,
                )
            )
        for copy in copies:
            copy.start()
        for copy in copies:
            copy.wait_recv()
        result = use(dst)
        return copies, result

    def summed(own):
        def use(dst):
            value = own
            for d in range(1, 8):
                value = value + dst[d]
            return value

        return use

    copies_y, sum_y = exchange("gy", 0, lambda peer: parts.at[peer], got_y, summed(parts[gy]))
    total_yz[0] = sum_y
    copies_z, sum_z = exchange("gz", 8, lambda peer: total_yz.at[0], got_z, summed(sum_y))
    total_yz[1] = sum_z

    def lower(dst):
        value = sum_z
        for d in range(1, 8):
            value = value + jnp.where(gx >= d, dst[d], 0.0)
        return value

    copies_x, sum_x = exchange("gx", 16, lambda peer: total_yz.at[1], got_x, lower)

    first = jnp.broadcast_to(onsets[pl.ds(gy // 4, 1), :], (8, 128))
    first = pltpu.roll(first, lax.rem(128 - 32 * lax.rem(gy, 4), 128), 1)
    first = jnp.where(lane < 32, first, 0)
    first = first + pltpu.roll(first, 32, 1)
    first = first + pltpu.roll(first, 64, 1)
    value = jnp.broadcast_to(sum_x, (8, 128))
    value = jnp.where((lane >> 5) >= first, value, 0.0)
    value = value + jnp.where(lane >= 32, pltpu.roll(value, 32, 1), 0.0)
    value = value + jnp.where(lane >= 64, pltpu.roll(value, 64, 1), 0.0)
    value = value * (0.25 * 256 / (nx * 16 * ny * 16 * nz * 128))
    value = pltpu.roll(value, lax.rem(128 - 4 * gz, 128), 1)
    value = by_step(value, (0, 96, 64, 32))
    energy_out[0] = value[0:4, 0:4]

    for has, copy in sends:

        @pl.when(has)
        def _(copy=copy):
            copy.wait_send()

    for copy in copies_y + copies_z + copies_x:
        copy.wait_send()
    for store in stores:
        store.wait()


def solution(mesh):
    sizes = tuple(mesh.shape[a] for a in ("gx", "gy", "gz"))

    def body(strain, cell_shell_index, onset_step):
        run = pl.pallas_call(
            lambda *refs: kernel(sizes, *refs),
            out_shape=(
                jax.ShapeDtypeStruct((8, 16, 16, 128), F32),
                jax.ShapeDtypeStruct((1, 4, 4), F32),
            ),
            in_specs=[pl.BlockSpec(memory_space=pltpu.HBM)] * 3,
            out_specs=(
                pl.BlockSpec(memory_space=pltpu.HBM),
                pl.BlockSpec(memory_space=pltpu.VMEM),
            ),
            scratch_shapes=[
                pltpu.VMEM((20, 20, 8, 128), F32),
                pltpu.VMEM((16, 16, 128), jnp.int32),
                pltpu.VMEM((2, 128), jnp.int32),
                pltpu.VMEM((8, 8, 128), F32),
                pltpu.VMEM((10, 8, 128), F32),
                pltpu.VMEM((10, 8, 128), F32),
                pltpu.VMEM((16, 20, 8, 128), F32),
                pltpu.VMEM((16, 16, 8, 128), F32),
                pltpu.VMEM((16, 16, 8, 128), F32),
                pltpu.VMEM((64, 128), F32),
                pltpu.VMEM((8, 1, 128), F32),
                pltpu.VMEM((8, 1, 128), F32),
                pltpu.VMEM((8, 1, 128), F32),
                pltpu.VMEM((8, 1, 128), F32),
                pltpu.VMEM((2, 1, 128), F32),
                pltpu.SemaphoreType.DMA((10,)),
                pltpu.SemaphoreType.DMA((8,)),
                pltpu.SemaphoreType.DMA((10,)),
                pltpu.SemaphoreType.DMA((10,)),
                pltpu.SemaphoreType.DMA((24,)),
                pltpu.SemaphoreType.DMA((24,)),
            ],
            compiler_params=pltpu.CompilerParams(collective_id=0, has_side_effects=True),
        )
        psi_four, energy = run(
            strain.reshape(8, 16, 16, 128), cell_shell_index, onset_step.reshape(2, 128)
        )
        return psi_four.reshape(strain.shape), energy

    placed = (P(None, None, "gx", "gy", "gz"), P("gx", "gy", "gz"), P())
    return jax.shard_map(
        body,
        mesh=mesh,
        in_specs=placed,
        out_specs=(P(None, None, "gx", "gy", "gz"), P("gx", None, ("gy", "gz"))),
        check_vma=False,
    )
```

time: 174 us -> 44.8 us (0.26)
  Pallas kernels: 0 us -> 41.1 us
  local copies, waits for them, and re-layouts: 40.3 us -> 2.85 us
  starting transfers between devices: 34.2 us -> 0 us
  loops' own time: 30.1 us -> 0 us
  blocking collectives: 23.2 us -> 0 us
  other arithmetic: 22.4 us -> 0 us
  matrix products: 12.8 us -> 0 us
  waiting for transfers between devices: 8.51 us -> 0 us
    pallas_call x0 -> x1, Pallas kernels: none -> 41.1 us  [body(): run(strain.reshape(8, 16, 16, 128), cell_shell_index, onset_step.reshape(...]
    another operation x1 -> x0, loops' own time: 30.1 us -> none  [body(): lax.scan(bin_plane, jnp.zeros((steps_count, shell_count), jnp.float32), (...]
    dynamic_slice x48 -> x0, local copies, waits for them, and re-layouts: 24.6 us -> none  [the longest x32 24.1 us: body(): lax.scan(bin_plane, jnp.zeros((steps_count, shell_count), jnp.float32), (...]
    ppermute x8 -> x0, starting transfers between devices: 23.6 us -> none  [the longest x3 13.6 us: extended(): lax.ppermute(last, axis, up)]
    all_to_all x1 -> x0, blocking collectives: 23.2 us -> none  [sent_and_summed(): lax.all_to_all(blocks, axis, split_axis=0, concat_axis=0, tiled=True)]
    dot_general x16 -> x0, matrix products: 12.8 us -> none  [bin_plane(): jnp.dot(flux_piece, one_hot, precision=lax.Precision.HIGHEST)]
    all_to_all x1 -> x0, starting transfers between devices: 10.6 us -> none  [sent_to_all(): lax.all_to_all(jnp.broadcast_to(value[None], (peers, *value.shape)), axis...]
    slice x1 -> x0, other arithmetic: 8.74 us -> none  [along_z(): views[offset] = padded[:, :, :, :, 2 + offset:2 + offset + cells_z]]
  transfers between devices with their start and end apart: 9 -> 0, of which waited for: 3 -> 0; matrix products, arithmetic and copies ran while one was open for 9% -> 0% of each run, Pallas kernels for 0% -> 0%
where the time goes in v1:
time: 44.8 us; the launch traced here: 44.6 us
  Pallas kernels  41.1 us (92%)
  local copies, waits for them, and re-layouts  2.85 us (6%)
  between operations  0.65 us (1%)
    pallas_call x1, Pallas kernels, body(): run(strain.reshape(8, 16, 16, 128), cell_shell_index, onset_step.reshape(...  41.1 us
    unnamed x4, local copies, waits for them, and re-layouts  2.85 us

profile of v1, /device:TPU:1, one launch (start us, length us, event | category | flops | bytes accessed | tf_op | source)
XLA Modules:
  0.0 44.6 jit_solution(13874329178428414012)
XLA Ops:
  0.6 41.1 %shard_map.50 = (f32[8,16,16,128]{3,2,1,0:T(8,128)}, f32[1,4,4]{2,1,0:T(4,128)}) custom-call(f32[8,16,16,128]{3,2,1,0:T(8,128)} %bitcast.3, s32[16,16,128]{2,1,0:T(8,128)} %refs_1_.1, s32[2,128]{1,0:T(2,128)} %bitcast.5), custom_call_target="tpu_custom_call" | custom-call | tf_op jit(solution)/shard_map/pallas_call | solution.py:364
  41.7 0.0 copy-start
  41.8 2.3 %copy.7 = f32[2,4,16,16,128]{4,3,2,1,0:T(8,128)} copy(f32[2,4,16,16,128]{4,3,2,1,0:T(8,128)} %bitcast.4) | data formatting | bytes 2097152
  44.0 0.0 copy-done
  44.0 0.6 %copy.8 = f32[1,4,4]{2,1,0:T(4,128)} copy(f32[1,4,4]{2,1,0:T(4,128)S(1)} %copy-done) | data formatting | bytes 128
Async XLA Ops:
  41.7 2.3 %copy-start = (f32[1,4,4]{2,1,0:T(4,128)S(1)}, f32[1,4,4]{2,1,0:T(4,128)}, u32[]{:S(2)}) copy-start(f32[1,4,4]{2,1,0:T(4,128)} %get-tuple-element.9) | copy-start | bytes 196

commit v2 on v1

v2 whole, which is shorter than its diff:
```python
import jax
import jax.numpy as jnp
from jax import lax
from jax.experimental import pallas as pl
from jax.experimental.pallas import tpu as pltpu
from jax.sharding import PartitionSpec as P

MESH = pl.DeviceIdType.MESH
F32 = jnp.float32
CT = 8


def kernel(
    sizes,
    strain,
    shells,
    onset,
    psi_out,
    energy_out,
    field,
    shell,
    onsets,
    zmid,
    zlow,
    zhigh,
    edge,
    firsts,
    seconds,
    binned,
    parts,
    got_y,
    got_z,
    got_x,
    summed,
    in_sem,
    halo_send,
    halo_recv,
    sum_send,
    sum_recv,
    know,
):
    nx, ny, nz = sizes
    gx, gy, gz = (lax.axis_index(a) for a in ("gx", "gy", "gz"))
    no = jnp.logical_not
    both = jnp.logical_and

    loads = [
        pltpu.make_async_copy(strain.at[c], field.at[2:18, 2:18, c], in_sem.at[c]) for c in range(CT)
    ]
    loads.append(pltpu.make_async_copy(shells, shell, in_sem.at[CT]))
    loads.append(pltpu.make_async_copy(onset, onsets, in_sem.at[CT + 1]))
    for load in loads:
        load.start()

    def when(cond, act):
        if cond is None:
            act()
        else:
            pl.when(cond)(act)

    def tell(sem, peer, cond=None):
        when(cond, lambda: pl.semaphore_signal(sem, inc=1, device_id=peer, device_id_type=MESH))

    def hear(sem, cond=None):
        when(cond, lambda: pl.semaphore_wait(sem, 1))

    def ring(axis, step):
        n = {"gy": ny, "gz": nz}[axis]
        return {axis: lax.rem({"gy": gy, "gz": gz}[axis] + (step + n), n)}

    barrier = pltpu.get_barrier_semaphore()
    x_lo, x_hi = gx > 0, gx < nx - 1
    y_lo, y_hi = gy > 0, gy < ny - 1
    z_lo, z_hi = gz > 0, gz < nz - 1
    tell(barrier, {"gx": gx - 1}, x_lo)
    tell(barrier, {"gx": gx + 1}, x_hi)
    for axis in ("gy", "gz"):
        for step in (-1, 1):
            tell(barrier, ring(axis, step))
    ll, lh, hl, hh = both(y_lo, z_lo), both(y_lo, z_hi), both(y_hi, z_lo), both(y_hi, z_hi)
    diagonal = {
        "ll": (ll, {"gy": gy - 1, "gz": gz - 1}),
        "lh": (lh, {"gy": gy - 1, "gz": gz + 1}),
        "hl": (hl, {"gy": gy + 1, "gz": gz - 1}),
        "hh": (hh, {"gy": gy + 1, "gz": gz + 1}),
    }
    for cond, peer in diagonal.values():
        tell(barrier, peer, cond)
    greeted = 4
    for cond in (x_lo, x_hi, ll, lh, hl, hh):
        greeted = greeted + cond.astype(jnp.int32)

    def zero(cond, ref):
        @pl.when(cond)
        def _():
            ref[...] = jnp.zeros(ref.shape, F32)

    zero(no(x_lo), field.at[0:2, 2:18])
    zero(no(x_hi), field.at[18:20, 2:18])
    zero(no(y_lo), field.at[2:18, 0:2])
    zero(no(y_hi), field.at[2:18, 18:20])
    zero(no(y_lo), zmid.at[0])
    zero(no(y_hi), zmid.at[9])
    zero(no(z_lo), zlow.at[1:9])
    zero(no(z_hi), zhigh.at[1:9])
    zero(no(ll), zlow.at[0])
    zero(no(lh), zhigh.at[0])
    zero(no(hl), zlow.at[9])
    zero(no(hh), zhigh.at[9])

    lane = lax.broadcasted_iota(jnp.int32, (8, 128), 1)
    sub = lax.broadcasted_iota(jnp.int32, (8, 128), 0)
    slot_of = ((lane + 2) & 127) >> 2
    quarter = lane & 3

    for load in loads:
        load.wait()

    packed = [jnp.zeros((8, 128), F32) for _ in range(8)]
    for s in range(32):
        mine = slot_of == s
        for b in range(8):
            row = field[s // 2 + 2, 2 * b + s % 2 + 2]
            moved = pltpu.roll(row, 4 * s, 1) if s else row
            packed[b] = jnp.where(mine, moved, packed[b])
    for b in range(8):
        zmid[b + 1] = packed[b]

    pl.semaphore_wait(barrier, greeted)

    halos = []

    def halo(sent, src, dst, peer, came):
        i = len(halos)
        copy = pltpu.make_async_remote_copy(
            src_ref=src,
            dst_ref=dst,
            send_sem=halo_send.at[i],
            recv_sem=halo_recv.at[i],
            device_id=peer,
            device_id_type=MESH,
        )
        halos.append((sent, copy, came))

    halo(z_hi, zmid.at[1:9], zlow.at[1:9], {"gz": gz + 1}, z_lo)
    halo(z_lo, zmid.at[1:9], zhigh.at[1:9], {"gz": gz - 1}, z_hi)
    halo(hh, zmid.at[8], zlow.at[0], diagonal["hh"][1], ll)
    halo(hl, zmid.at[8], zhigh.at[0], diagonal["hl"][1], lh)
    halo(lh, zmid.at[1], zlow.at[9], diagonal["lh"][1], hl)
    halo(ll, zmid.at[1], zhigh.at[9], diagonal["ll"][1], hh)
    halo(y_hi, zmid.at[8], zmid.at[0], {"gy": gy + 1}, y_lo)
    halo(y_lo, zmid.at[1], zmid.at[9], {"gy": gy - 1}, y_hi)
    halo(y_hi, field.at[2:18, 16:18], field.at[2:18, 0:2], {"gy": gy + 1}, y_lo)
    halo(y_lo, field.at[2:18, 2:4], field.at[2:18, 18:20], {"gy": gy - 1}, y_hi)
    halo(x_hi, field.at[16:18, 2:18], field.at[0:2, 2:18], {"gx": gx + 1}, x_lo)
    halo(x_lo, field.at[2:4, 2:18], field.at[18:20, 2:18], {"gx": gx - 1}, x_hi)
    for sent, copy, _ in halos:
        when(sent, copy.start)

    for base, axis in ((0, "gy"), (4, "gz")):
        tell(know.at[base], ring(axis, -1))
        tell(know.at[base + 1], ring(axis, 1))
    tell(know.at[8], {"gx": gx - 1}, both(x_lo, x_hi))
    tell(know.at[9], {"gx": gx + 1}, both(x_lo, x_hi))

    def shifts(f):
        return (pltpu.roll(f, k, 1) for k in (127, 126, 1, 2))

    def along_z(i, _):
        for j in range(2):
            x = 2 * i + j
            for y in range(16):
                up1, up2, down1, down2 = shifts(field[x + 2, y + 2])
                firsts[x, y + 2] = 8.0 * (up1 - down1) - (up2 - down2)
                seconds[x, y] = 16.0 * (up1 + down1) - (up2 + down2)
        return 0

    lax.fori_loop(0, 8, along_z, 0)

    for base, axis in ((0, "gy"), (4, "gz")):
        hear(know.at[base])
        hear(know.at[base + 1])
        tell(know.at[base + 2], ring(axis, -2))
        tell(know.at[base + 3], ring(axis, 2))
    hear(know.at[8], gx + 2 < nx)
    hear(know.at[9], gx >= 2)
    tell(know.at[10], {"gx": gx - 2}, both(gx >= 2, x_hi))
    tell(know.at[11], {"gx": gx + 2}, both(gx + 2 < nx, x_lo))

    def arrive(i):
        when(halos[i][2], halos[i][1].wait_recv)

    for i in range(8):
        arrive(i)

    signs = jnp.where(sub < 4, 1.0 / 24.0, -1.0 / 24.0).astype(F32)
    ups, downs, errors = [], [], []
    bends = []
    for b in range(10):
        wrong = jnp.where(quarter >= 2, zlow[b], zhigh[b]) - zmid[b]
        near = jnp.where(
            quarter == 0, pltpu.roll(wrong, 1, 1), jnp.where(quarter == 3, pltpu.roll(wrong, 127, 1), 0.0)
        )
        far = jnp.where(quarter < 2, pltpu.roll(wrong, 2, 1), pltpu.roll(wrong, 126, 1))
        slope = far - 8.0 * near
        slope = jnp.where(quarter < 2, slope, -slope)
        errors.append(slope)
        ups.append(pltpu.roll(slope, 124, 1))
        downs.append(pltpu.roll(slope, 4, 1))
        bends.append(16.0 * near - far)
    even = (slot_of & 1) == 0
    for b in range(1, 9):
        step1 = jnp.where(even, ups[b] - ups[b - 1], downs[b + 1] - downs[b])
        mixed = 8.0 * step1 - (errors[b + 1] - errors[b - 1])
        edge[b - 1] = -(bends[b] * signs) - pltpu.roll(mixed, 4, 0) * (1.0 / 144.0)

    step_of = sub & 3
    at_end = jnp.logical_or(lane < 2, lane >= 126)
    uz = (lane + gz * 128).astype(F32)
    uz = (uz + 0.5) / (nz * 128) - 0.5
    uz2 = uz * uz + 0.05

    def rows(xs, ys, total):
        lefts, rights = [], []
        for x in xs:
            ux = (x + gx * 16).astype(F32)
            ux = (ux + 0.5) / (nx * 16) - 0.5
            ux2 = uz2 + ux * ux
            for y in ys:
                f = field[x + 2, y + 2]
                near = (field[x + 1, y + 2] + field[x + 3, y + 2]) + (field[x + 2, y + 1] + field[x + 2, y + 3])
                far = (field[x, y + 2] + field[x + 4, y + 2]) + (field[x + 2, y] + field[x + 2, y + 4])
                combo = (16.0 * near - far) - (seconds[x, y] + 30.0 * f)
                mixed = 8.0 * (firsts[x, y + 3] - firsts[x, y + 1]) - (firsts[x, y + 4] - firsts[x, y])
                end = pltpu.roll(edge[y // 2], 128 - 4 * (2 * x + y % 2), 1)
                value = combo * signs - pltpu.roll(mixed, 4, 0) * (1.0 / 144.0)
                value = value + jnp.where(at_end, end, 0.0)
                psi_out[x, y] = value
                news = value + jnp.where(step_of >= 1, pltpu.roll(value, 1, 0), 0.0)
                news = news + jnp.where(step_of >= 2, pltpu.roll(news, 2, 0), 0.0)
                power = news * news
                power = power + pltpu.roll(power, 4, 0)
                uy = (gy * 16 + y).astype(F32)
                uy = (uy + 0.5) / (ny * 16) - 0.5
                flux = power * ((ux2 + uy * uy) * 0.0625)
                high = flux.astype(jnp.bfloat16).astype(F32)
                split = jnp.where(sub < 4, high, flux - high)
                label = jnp.broadcast_to(shell[x, pl.ds(y, 1), :], (8, 128))
                outer = label >> 5
                inner = label & 31
                lefts.append(
                    jnp.concatenate([jnp.where(outer == k, split, 0.0) for k in range(8)], axis=0)
                )
                rights.append(
                    jnp.concatenate(
                        [jnp.where(inner == sub + 8 * j, 1.0, 0.0).astype(F32) for j in range(4)], axis=0
                    )
                )
        left = jnp.concatenate(lefts, axis=1)
        right = jnp.concatenate(rights, axis=1)
        return total + lax.dot_general(
            left, right, (((1,), (1,)), ((), ())), preferred_element_type=F32
        )

    total = jnp.zeros((64, 32), F32)
    total = lax.fori_loop(2, 14, lambda x, t: rows([x], range(2, 14), t), total)

    for i in range(8, 12):
        arrive(i)

    def along_z_ends(i, _):
        for j in range(8):
            x = 8 * i + j
            for y in (0, 1, 18, 19):
                up1, up2, down1, down2 = shifts(field[x + 2, y])
                firsts[x, y] = 8.0 * (up1 - down1) - (up2 - down2)
        return 0

    lax.fori_loop(0, 2, along_z_ends, 0)

    total = lax.fori_loop(
        0, 3, lambda i, t: rows([4 * i + 2 + j for j in range(4)], (0, 1, 14, 15), t), total
    )
    total = lax.fori_loop(
        0, 4, lambda i, t: rows([i + 12 * (i // 2)], range(16), t), total
    )

    for base in (0, 4):
        hear(know.at[base + 2])
        hear(know.at[base + 3])
    hear(know.at[10], gx + 3 < nx)
    hear(know.at[11], gx >= 3)
    tell(know.at[12], {"gx": gx - 4}, both(gx >= 4, x_hi))

    def by_step(x, moves):
        moved = x
        for t in range(1, 4):
            moved = jnp.where(step_of == t, pltpu.roll(x, moves[t], 1), moved)
        return moved

    binned[...] = jnp.zeros((64, 128), F32)
    binned[:, 0:32] = total
    for k in range(8):
        spread = by_step(binned[8 * k : 8 * k + 8, :], (0, 32, 64, 96))
        parts[k] = jnp.sum(spread, axis=0, keepdims=True)

    sums = []

    def pass_on(i, sent, src, dst, peer, came):
        copy = pltpu.make_async_remote_copy(
            src_ref=src,
            dst_ref=dst,
            send_sem=sum_send.at[i],
            recv_sem=sum_recv.at[i],
            device_id=peer,
            device_id_type=MESH,
        )
        sums.append((sent, copy))
        when(sent, copy.start)
        return lambda: when(came, copy.wait_recv)

    waits = []
    for d in range(1, ny):
        peer = ring("gy", d)
        waits.append(pass_on(d, None, parts.at[peer["gy"]], got_y.at[d], peer, None))
    for wait in waits:
        wait()
    value = parts[gy]
    for d in range(1, ny):
        value = value + got_y[d]

    summed[0] = value
    waits = [pass_on(8 + d, None, summed.at[0], got_z.at[d], ring("gz", d), None) for d in range(1, nz)]
    for wait in waits:
        wait()
    for d in range(1, nz):
        value = value + got_z[d]

    summed[1] = value
    hear(know.at[12], gx + 5 < nx)
    waits = [
        pass_on(16 + d, gx + d < nx, summed.at[1], got_x.at[d], {"gx": gx + d}, gx >= d)
        for d in range(1, nx)
    ]
    for wait in waits:
        wait()
    for d in range(1, nx):
        value = value + jnp.where(gx >= d, got_x[d], 0.0)

    first = jnp.broadcast_to(onsets[pl.ds(gy // 4, 1), :], (8, 128))
    first = pltpu.roll(first, lax.rem(128 - 32 * lax.rem(gy, 4), 128), 1)
    first = jnp.where(lane < 32, first, 0)
    first = first + pltpu.roll(first, 32, 1)
    first = first + pltpu.roll(first, 64, 1)
    value = jnp.broadcast_to(value, (8, 128))
    value = jnp.where((lane >> 5) >= first, value, 0.0)
    value = value + jnp.where(lane >= 32, pltpu.roll(value, 32, 1), 0.0)
    value = value + jnp.where(lane >= 64, pltpu.roll(value, 64, 1), 0.0)
    value = value * (0.25 * 256 / (nx * 16 * ny * 16 * nz * 128))
    value = pltpu.roll(value, lax.rem(128 - 4 * gz, 128), 1)
    value = by_step(value, (0, 96, 64, 32))
    energy_out[0] = value[0:4, 0:4]

    for sent, copy, _ in halos:
        when(sent, copy.wait_send)
    for sent, copy in sums:
        when(sent, copy.wait_send)


def write(psi, energy, psi_out, energy_out, sem):
    copies = [pltpu.make_async_copy(psi.at[:, :, c], psi_out.at[c], sem.at[c]) for c in range(CT)]
    copies.append(pltpu.make_async_copy(energy, energy_out, sem.at[CT]))
    for copy in copies:
        copy.start()
    for copy in copies:
        copy.wait()


def solution(mesh):
    sizes = tuple(mesh.shape[a] for a in ("gx", "gy", "gz"))
    vmem = pl.BlockSpec(memory_space=pltpu.VMEM)
    hbm = pl.BlockSpec(memory_space=pltpu.HBM)

    def body(strain, cell_shell_index, onset_step):
        psi, energy = pl.pallas_call(
            lambda *refs: kernel(sizes, *refs),
            out_shape=(pltpu.VMEM((16, 16, 8, 128), F32), pltpu.VMEM((1, 4, 4), F32)),
            in_specs=[hbm] * 3,
            out_specs=(vmem, vmem),
            scratch_shapes=[
                pltpu.VMEM((20, 20, 8, 128), F32),
                pltpu.VMEM((16, 16, 128), jnp.int32),
                pltpu.VMEM((2, 128), jnp.int32),
                pltpu.VMEM((10, 8, 128), F32),
                pltpu.VMEM((10, 8, 128), F32),
                pltpu.VMEM((10, 8, 128), F32),
                pltpu.VMEM((8, 8, 128), F32),
                pltpu.VMEM((16, 20, 8, 128), F32),
                pltpu.VMEM((16, 16, 8, 128), F32),
                pltpu.VMEM((64, 128), F32),
                pltpu.VMEM((8, 1, 128), F32),
                pltpu.VMEM((8, 1, 128), F32),
                pltpu.VMEM((8, 1, 128), F32),
                pltpu.VMEM((8, 1, 128), F32),
                pltpu.VMEM((2, 1, 128), F32),
                pltpu.SemaphoreType.DMA((10,)),
                pltpu.SemaphoreType.DMA((12,)),
                pltpu.SemaphoreType.DMA((12,)),
                pltpu.SemaphoreType.DMA((24,)),
                pltpu.SemaphoreType.DMA((24,)),
                pltpu.SemaphoreType.REGULAR((13,)),
            ],
            compiler_params=pltpu.CompilerParams(collective_id=0, has_side_effects=True),
        )(strain.reshape(8, 16, 16, 128), cell_shell_index, onset_step.reshape(2, 128))
        psi_four, energy = pl.pallas_call(
            write,
            out_shape=(
                jax.ShapeDtypeStruct((8, 16, 16, 128), F32),
                jax.ShapeDtypeStruct((1, 4, 4), F32),
            ),
            in_specs=[vmem] * 2,
            out_specs=(hbm, hbm),
            scratch_shapes=[pltpu.SemaphoreType.DMA((CT + 1,))],
        )(*(pltpu.with_memory_space_constraint(a, pltpu.VMEM) for a in (psi, energy)))
        return psi_four.reshape(strain.shape), energy

    placed = (P(None, None, "gx", "gy", "gz"), P("gx", "gy", "gz"), P())
    return jax.shard_map(
        body,
        mesh=mesh,
        in_specs=placed,
        out_specs=(P(None, None, "gx", "gy", "gz"), P("gx", None, ("gy", "gz"))),
        check_vma=False,
    )
```

time: 44.8 us -> 29.4 us (0.66)
  the two profiles are of different devices: /device:TPU:1 before, /device:TPU:384 now
where the time goes in v2:
time: 29.4 us; the launch traced here: 29.3 us
  Pallas kernels  28.7 us (98%)
  between operations  0.64 us (2%)
    pallas_call x1, Pallas kernels, body(): pl.pallas_call(lambda *refs: kernel(sizes, *refs), out_shape=(pltpu.VMEM(...  27.6 us
    pallas_call x1, Pallas kernels, body(): pl.pallas_call(write, out_shape=(jax.ShapeDtypeStruct((8, 16, 16, 128), F...  1.04 us

profile of v2, /device:TPU:384, one launch (start us, length us, event | category | flops | bytes accessed | tf_op | source)
XLA Modules:
  0.0 29.3 jit_solution(12333069026805729596)
XLA Ops:
  0.6 27.6 %shard_map.50 = (f32[16,16,8,128]{3,2,1,0:T(8,128)S(1)}, f32[1,4,4]{2,1,0:T(4,128)S(1)}) custom-call(f32[8,16,16,128]{3,2,1,0:T(8,128)} %bitcast.3, s32[16,16,128]{2,1,0:T(8,128)} %refs_1_.1, s32[2,128]{1,0:T(2,128)} %bitcast.4), custom_call_target="tpu_custom_call" | custom-call | tf_op jit(solution)/shard_map/pallas_call | solution.py:385
  28.2 1.0 %shard_map.51 = (f32[8,16,16,128]{3,2,1,0:T(8,128)}, f32[1,4,4]{2,1,0:T(4,128)}) custom-call(f32[16,16,8,128]{3,2,1,0:T(8,128)S(1)} %get-tuple-element.6.psi, f32[1,4,4]{2,1,0:T(4,128)S(1)} %get-tuple-element.7.energy), custom_call_target="tpu_custom_call" | custom-call | tf_op jit(solution)/shard_map/pallas_call | solution.py:415

commit v3 on v2

v3 whole, which is shorter than its diff:
```python
import jax
import jax.numpy as jnp
from jax import lax
from jax.experimental import pallas as pl
from jax.experimental.pallas import tpu as pltpu
from jax.sharding import PartitionSpec as P

MESH = pl.DeviceIdType.MESH
F32 = jnp.float32
CT = 8


def kernel(
    sizes,
    strain,
    shells,
    onset,
    psi_out,
    energy_out,
    field,
    shell,
    onsets,
    zmid,
    zlow,
    zhigh,
    outer,
    inner,
    firsts,
    seconds,
    binned,
    parts,
    got,
    got_x,
    summed,
    in_sem,
    sent_sem,
    came_sem,
    know,
):
    nx, ny, nz = sizes
    gx, gy, gz = (lax.axis_index(a) for a in ("gx", "gy", "gz"))
    no = jnp.logical_not
    both = jnp.logical_and

    for h in range(2):
        for c in range(CT):
            pltpu.make_async_copy(
                strain.at[c, 8 * h : 8 * h + 8],
                field.at[8 * h + 2 : 8 * h + 10, 2:18, c],
                in_sem.at[h],
            ).start()
    labels = pltpu.make_async_copy(shells, shell, in_sem.at[2])
    starts = pltpu.make_async_copy(onset, onsets, in_sem.at[3])
    labels.start()
    starts.start()

    def when(cond, act):
        if cond is None:
            act()
        else:
            pl.when(cond)(act)

    def tell(sem, peer, cond=None):
        when(cond, lambda: pl.semaphore_signal(sem, inc=1, device_id=peer, device_id_type=MESH))

    def total_of(conds):
        return sum(c.astype(jnp.int32) for c in conds)

    def near_to(dy, dz):
        peer = {}
        if dy:
            peer["gy"] = lax.rem(gy + (dy + ny), ny)
        if dz:
            peer["gz"] = lax.rem(gz + (dz + nz), nz)
        return peer

    around = [(dy, dz) for dy in (-1, 0, 1) for dz in (-1, 0, 1) if dy or dz]

    barrier = pltpu.get_barrier_semaphore()
    x_lo, x_hi = gx > 0, gx < nx - 1
    y_lo, y_hi = gy > 0, gy < ny - 1
    z_lo, z_hi = gz > 0, gz < nz - 1
    half = nx // 2
    late = both(x_hi, gx < half)
    tell(barrier, {"gx": gx - 1}, gx > half)
    for step in around:
        tell(barrier, near_to(*step))
    for d in range(1, nx):
        tell(barrier, {"gx": gx + d}, gx + d < nx)
    greeted = 8 + gx + total_of((both(x_hi, gx >= half),))

    def zero(cond, ref):
        @pl.when(cond)
        def _():
            ref[...] = jnp.zeros(ref.shape, F32)

    zero(no(x_lo), field.at[0:2, 2:18])
    zero(no(x_hi), field.at[18:20, 2:18])

    lane = lax.broadcasted_iota(jnp.int32, (8, 128), 1)
    sub = lax.broadcasted_iota(jnp.int32, (8, 128), 0)
    slot_of = ((lane + 2) & 127) >> 2
    quarter = lane & 3

    packed = [jnp.zeros((8, 128), F32) for _ in range(8)]
    for s in range(32):
        if s % 16 == 0:
            own = field.at[s // 2 + 2 : s // 2 + 10, 2:18]
            pltpu.make_async_copy(own, own, in_sem.at[s // 16]).wait()
        mine = slot_of == s
        for b in range(8):
            row = field[s // 2 + 2, 2 * b + s % 2 + 2]
            moved = pltpu.roll(row, 4 * s, 1) if s else row
            packed[b] = jnp.where(mine, moved, packed[b])
    for b in range(8):
        zmid[b + 1] = packed[b]

    pl.semaphore_wait(barrier, greeted)

    def remote(src, dst, send, recv, peer):
        return pltpu.make_async_remote_copy(
            src_ref=src, dst_ref=dst, send_sem=send, recv_sem=recv, device_id=peer, device_id_type=MESH
        )

    z_halos = [
        (zmid.at[1:9], zlow.at[1:9], (0, 1)),
        (zmid.at[1:9], zhigh.at[1:9], (0, -1)),
        (zmid.at[8], zlow.at[0], (1, 1)),
        (zmid.at[8], zhigh.at[0], (1, -1)),
        (zmid.at[1], zlow.at[9], (-1, 1)),
        (zmid.at[1], zhigh.at[9], (-1, -1)),
        (zmid.at[8], zmid.at[0], (1, 0)),
        (zmid.at[1], zmid.at[9], (-1, 0)),
    ]
    y_halos = [
        (field.at[2:18, 16:18], field.at[2:18, 0:2], (1, 0)),
        (field.at[2:18, 2:4], field.at[2:18, 18:20], (-1, 0)),
    ]
    for i, group in enumerate((z_halos, y_halos)):
        for src, dst, step in group:
            remote(src, dst, sent_sem.at[i], came_sem.at[i], near_to(*step)).start()
    x_down = remote(
        field.at[2:4, 2:18], field.at[18:20, 2:18], sent_sem.at[2], came_sem.at[2], {"gx": gx - 1}
    )
    x_up = remote(
        field.at[16:18, 2:18], field.at[0:2, 2:18], sent_sem.at[3], came_sem.at[3], {"gx": gx + 1}
    )
    when(x_lo, x_down.start)
    when(both(x_hi, gx >= half), x_up.start)

    tell(know.at[0], {"gx": gx - 1}, both(x_lo, gx <= half))
    for step in around:
        tell(know.at[1], near_to(*step))
    for d in range(1, nx):
        tell(know.at[3], {"gx": gx - d}, gx >= d)

    labels.wait()
    starts.wait()
    outer[...] = shell[...] >> 5
    inner[...] = shell[...] & 31
    first = jnp.broadcast_to(onsets[pl.ds(gy // 4, 1), :], (8, 128))
    first = pltpu.roll(first, lax.rem(128 - 32 * lax.rem(gy, 4), 128), 1)
    first = jnp.where(lane < 32, first, 0)
    first = first + pltpu.roll(first, 32, 1)
    first = first + pltpu.roll(first, 64, 1)

    signs = jnp.where(sub < 4, 1.0 / 24.0, -1.0 / 24.0).astype(F32)
    minus = -signs

    def shifts(f):
        return (pltpu.roll(f, k, 1) for k in (127, 126, 1, 2))

    def slope(up1, up2, down1, down2):
        d = (up1 - down1) * (8.0 / 144.0) - (up2 - down2) * (1.0 / 144.0)
        return pltpu.roll(d, 4, 0)

    def along_z(i, _):
        for j in range(2):
            x = 2 * i + j
            for y in range(16):
                f = field[x + 2, y + 2]
                up1, up2, down1, down2 = shifts(f)
                firsts[x, y + 2] = slope(up1, up2, down1, down2)
                bend = 16.0 * (up1 + down1) - (up2 + down2)
                seconds[x, y] = (bend + 30.0 * f) * minus
        return 0

    lax.fori_loop(0, 8, along_z, 0)

    pl.semaphore_wait(know.at[1], 8)
    for dy, dz in around:
        tell(know.at[2], near_to(2 * dy, 2 * dz))

    when(late, lambda: pl.semaphore_wait(know.at[0], 1))
    when(late, x_up.start)

    def arrive(i, ref):
        pltpu.make_async_copy(ref, ref, came_sem.at[i]).wait()

    arrive(0, field.at[0:2, 0:11])

    ups, downs, errors = [], [], []
    bends = []
    for b in range(10):
        low, high, mid = zlow[b], zhigh[b], zmid[b]
        in_y = {0: y_lo, 9: y_hi}.get(b)
        has_low, has_high = z_lo, z_hi
        if in_y is not None:
            has_low, has_high = both(z_lo, in_y), both(z_hi, in_y)
            mid = jnp.where(in_y, mid, 0.0)
        low, high = jnp.where(has_low, low, 0.0), jnp.where(has_high, high, 0.0)
        wrong = jnp.where(quarter >= 2, low, high) - mid
        near = jnp.where(
            quarter == 0, pltpu.roll(wrong, 1, 1), jnp.where(quarter == 3, pltpu.roll(wrong, 127, 1), 0.0)
        )
        far = jnp.where(quarter < 2, pltpu.roll(wrong, 2, 1), pltpu.roll(wrong, 126, 1))
        error = far - 8.0 * near
        error = jnp.where(quarter < 2, error, -error)
        errors.append(error)
        ups.append(pltpu.roll(error, 124, 1))
        downs.append(pltpu.roll(error, 4, 1))
        bends.append(16.0 * near - far)
    even = (slot_of & 1) == 0
    at_end = jnp.logical_or(lane < 2, lane >= 126)
    for b in range(1, 9):
        step1 = jnp.where(even, ups[b] - ups[b - 1], downs[b + 1] - downs[b])
        mixed = 8.0 * step1 - (errors[b + 1] - errors[b - 1])
        fix = bends[b] * minus - pltpu.roll(mixed, 4, 0) * (1.0 / 144.0)
        for s in range(32):
            x, y = s // 2, 2 * b - 2 + s % 2
            end = pltpu.roll(fix, 128 - 4 * s, 1) if s else fix
            seconds[x, y] = seconds[x, y] + jnp.where(at_end, end, 0.0)

    step_of = sub & 3
    uz = (lane + gz * 128).astype(F32)
    uz = (uz + 0.5) / (nz * 128) - 0.5
    uz2 = (uz * uz + 0.05) * 0.0625

    def rows(xs, ys, total):
        lefts, rights = [], []
        for x in xs:
            ux = (x + gx * 16).astype(F32)
            ux = (ux + 0.5) / (nx * 16) - 0.5
            ux2 = uz2 + ux * ux * 0.0625
            for y in ys:
                near = (field[x + 1, y + 2] + field[x + 3, y + 2]) + (field[x + 2, y + 1] + field[x + 2, y + 3])
                far = (field[x, y + 2] + field[x + 4, y + 2]) + (field[x + 2, y] + field[x + 2, y + 4])
                mixed = 8.0 * (firsts[x, y + 3] - firsts[x, y + 1]) - (firsts[x, y + 4] - firsts[x, y])
                value = (16.0 * near - far) * signs + (seconds[x, y] - mixed)
                psi_out[x, y] = value
                news = value + jnp.where(step_of >= 1, pltpu.roll(value, 1, 0), 0.0)
                news = news + jnp.where(step_of >= 2, pltpu.roll(news, 2, 0), 0.0)
                power = news * news
                power = power + pltpu.roll(power, 4, 0)
                uy = (gy * 16 + y).astype(F32)
                uy = (uy + 0.5) / (ny * 16) - 0.5
                flux = power * (ux2 + uy * uy * 0.0625)
                high = flux.astype(jnp.bfloat16).astype(F32)
                split = jnp.where(sub < 4, high, flux - high)
                high_label = jnp.broadcast_to(outer[x, pl.ds(y, 1), :], (8, 128))
                low_label = jnp.broadcast_to(inner[x, pl.ds(y, 1), :], (8, 128))
                lefts.append(
                    jnp.concatenate([jnp.where(high_label == k, split, 0.0) for k in range(8)], axis=0)
                )
                rights.append(
                    jnp.concatenate(
                        [jnp.where(low_label == sub + 8 * j, 1.0, 0.0).astype(F32) for j in range(4)], axis=0
                    )
                )
        left = jnp.concatenate(lefts, axis=1)
        right = jnp.concatenate(rights, axis=1)
        return total + lax.dot_general(
            left, right, (((1,), (1,)), ((), ())), preferred_element_type=F32
        )

    total = jnp.zeros((64, 32), F32)
    total = lax.fori_loop(0, 4, lambda i, t: rows([3 * i + 2 + j for j in range(3)], range(2, 14), t), total)

    arrive(1, field.at[0:16, 0:4])
    when(x_hi, x_down.wait_recv)
    when(x_lo, x_up.wait_recv)
    zero(no(y_lo), field.at[2:18, 0:2])
    zero(no(y_hi), field.at[2:18, 18:20])

    def along_z_ends(i, _):
        for j in range(8):
            x = 8 * i + j
            for y in (0, 1, 18, 19):
                up1, up2, down1, down2 = shifts(field[x + 2, y])
                firsts[x, y] = slope(up1, up2, down1, down2)
        return 0

    lax.fori_loop(0, 2, along_z_ends, 0)

    total = rows(range(2, 14), (0, 1, 14, 15), total)
    total = lax.fori_loop(
        0, 2, lambda i, t: rows([14 * i, 14 * i + 1], range(16), t), total
    )

    pl.semaphore_wait(know.at[2], 8)

    def by_step(x, moves):
        moved = x
        for t in range(1, 4):
            moved = jnp.where(step_of == t, pltpu.roll(x, moves[t], 1), moved)
        return moved

    binned[...] = jnp.zeros((64, 128), F32)
    binned[:, 0:32] = total
    for k in range(8):
        spread = by_step(binned[8 * k : 8 * k + 8, :], (0, 32, 64, 96))
        parts[k] = jnp.sum(spread, axis=0, keepdims=True)

    offsets = [(dy, dz) for dy in range(ny) for dz in range(nz) if dy or dz]
    offsets.sort(key=lambda o: -(min(o[0], ny - o[0]) + min(o[1], nz - o[1]) / 2))
    for i, (dy, dz) in enumerate(offsets):
        peer = near_to(dy, dz)
        remote(parts.at[peer.get("gy", gy)], got.at[i], sent_sem.at[4], came_sem.at[4], peer).start()

    arrive(4, got)
    sums = [parts[gy]] + [got[i] for i in range(len(offsets))]
    while len(sums) > 1:
        sums = [a + b for a, b in zip(sums[::2], sums[1::2])]
    value = sums[0]

    summed[0] = value
    when(x_hi, lambda: pl.semaphore_wait(know.at[3], nx - 1 - gx))
    for d in range(1, nx):
        copy = remote(summed.at[0], got_x.at[d - 1], sent_sem.at[5], came_sem.at[5], {"gx": gx + d})
        when(gx + d < nx, copy.start)
    for n in range(1, nx):
        when(gx == n, lambda n=n: arrive(5, got_x.at[0:n]))
    for d in range(1, nx):
        value = value + jnp.where(gx >= d, got_x[d - 1], 0.0)

    value = jnp.broadcast_to(value, (8, 128))
    value = jnp.where((lane >> 5) >= first, value, 0.0)
    value = value * (0.25 * 256 / (nx * 16 * ny * 16 * nz * 128))
    steps = [pltpu.roll(value, lax.rem(256 - 32 * t - 4 * gz, 128), 1) for t in range(4)]
    value = steps[0]
    for t in range(1, 4):
        value = value + jnp.where(sub >= t, steps[t], 0.0)
    energy_out[0] = value[0:4, 0:4]

    def left(i, ref):
        pltpu.make_async_copy(ref, ref, sent_sem.at[i]).wait()

    left(0, field.at[0:2, 0:11])
    left(1, field.at[0:16, 0:4])
    when(x_lo, x_down.wait_send)
    when(x_hi, x_up.wait_send)
    left(4, got)
    for n in range(1, nx):
        when(gx == nx - 1 - n, lambda n=n: left(5, got_x.at[0:n]))


def write(psi, energy, psi_out, energy_out, sem):
    for c in range(CT):
        pltpu.make_async_copy(psi.at[:, :, c], psi_out.at[c], sem.at[0]).start()
    small = pltpu.make_async_copy(energy, energy_out, sem.at[1])
    small.start()
    pltpu.make_async_copy(psi_out, psi_out, sem.at[0]).wait()
    small.wait()


def solution(mesh):
    sizes = tuple(mesh.shape[a] for a in ("gx", "gy", "gz"))
    vmem = pl.BlockSpec(memory_space=pltpu.VMEM)
    hbm = pl.BlockSpec(memory_space=pltpu.HBM)

    def body(strain, cell_shell_index, onset_step):
        psi, energy = pl.pallas_call(
            lambda *refs: kernel(sizes, *refs),
            out_shape=(pltpu.VMEM((16, 16, 8, 128), F32), pltpu.VMEM((1, 4, 4), F32)),
            in_specs=[hbm] * 3,
            out_specs=(vmem, vmem),
            scratch_shapes=[
                pltpu.VMEM((20, 20, 8, 128), F32),
                pltpu.VMEM((16, 16, 128), jnp.int32),
                pltpu.VMEM((2, 128), jnp.int32),
                pltpu.VMEM((10, 8, 128), F32),
                pltpu.VMEM((10, 8, 128), F32),
                pltpu.VMEM((10, 8, 128), F32),
                pltpu.VMEM((16, 16, 128), jnp.int32),
                pltpu.VMEM((16, 16, 128), jnp.int32),
                pltpu.VMEM((16, 20, 8, 128), F32),
                pltpu.VMEM((16, 16, 8, 128), F32),
                pltpu.VMEM((64, 128), F32),
                pltpu.VMEM((8, 1, 128), F32),
                pltpu.VMEM((63, 1, 128), F32),
                pltpu.VMEM((7, 1, 128), F32),
                pltpu.VMEM((1, 1, 128), F32),
                pltpu.SemaphoreType.DMA((4,)),
                pltpu.SemaphoreType.DMA((6,)),
                pltpu.SemaphoreType.DMA((6,)),
                pltpu.SemaphoreType.REGULAR((4,)),
            ],
            compiler_params=pltpu.CompilerParams(collective_id=0, has_side_effects=True),
        )(strain.reshape(8, 16, 16, 128), cell_shell_index, onset_step.reshape(2, 128))
        psi_four, energy = pl.pallas_call(
            write,
            out_shape=(
                jax.ShapeDtypeStruct((8, 16, 16, 128), F32),
                jax.ShapeDtypeStruct((1, 4, 4), F32),
            ),
            in_specs=[vmem] * 2,
            out_specs=(hbm, hbm),
            scratch_shapes=[pltpu.SemaphoreType.DMA((2,))],
        )(*(pltpu.with_memory_space_constraint(a, pltpu.VMEM) for a in (psi, energy)))
        return psi_four.reshape(strain.shape), energy

    placed = (P(None, None, "gx", "gy", "gz"), P("gx", "gy", "gz"), P())
    return jax.shard_map(
        body,
        mesh=mesh,
        in_specs=placed,
        out_specs=(P(None, None, "gx", "gy", "gz"), P("gx", None, ("gy", "gz"))),
        check_vma=False,
    )
```

time: 29.4 us -> 24.5 us (0.83)
  the two profiles are of different devices: /device:TPU:384 before, /device:TPU:320 now
where the time goes in v3:
time: 24.5 us; the launch traced here: 24.4 us
  Pallas kernels  23.7 us (97%)
  between operations  0.64 us (3%)
    pallas_call x1, Pallas kernels, body(): pl.pallas_call(lambda *refs: kernel(sizes, *refs), out_shape=(pltpu.VMEM(...  22.7 us
    pallas_call x1, Pallas kernels, body(): pl.pallas_call(write, out_shape=(jax.ShapeDtypeStruct((8, 16, 16, 128), F...  0.98 us

profile of v3, /device:TPU:320, one launch (start us, length us, event | category | flops | bytes accessed | tf_op | source)
XLA Modules:
  0.0 24.4 jit_solution(433153962926150158)
XLA Ops:
  0.6 22.7 %shard_map.50 = (f32[16,16,8,128]{3,2,1,0:T(8,128)S(1)}, f32[1,4,4]{2,1,0:T(4,128)S(1)}) custom-call(f32[8,16,16,128]{3,2,1,0:T(8,128)} %bitcast.3, s32[16,16,128]{2,1,0:T(8,128)} %refs_1_.1, s32[2,128]{1,0:T(2,128)} %bitcast.4), custom_call_target="tpu_custom_call" | custom-call | tf_op jit(solution)/shard_map/pallas_call | solution.py:372
  23.4 1.0 %shard_map.51 = (f32[8,16,16,128]{3,2,1,0:T(8,128)}, f32[1,4,4]{2,1,0:T(4,128)}) custom-call(f32[16,16,8,128]{3,2,1,0:T(8,128)S(1)} %get-tuple-element.6.psi, f32[1,4,4]{2,1,0:T(4,128)S(1)} %get-tuple-element.7.energy), custom_call_target="tpu_custom_call" | custom-call | tf_op jit(solution)/shard_map/pallas_call | solution.py:400

commit v4 on v3

v4 whole, which is shorter than its diff:
```python
import jax
import jax.numpy as jnp
from jax import lax
from jax.experimental import pallas as pl
from jax.experimental.pallas import tpu as pltpu
from jax.sharding import PartitionSpec as P

MESH = pl.DeviceIdType.MESH
F32 = jnp.float32
CT = 8


def kernel(
    sizes,
    strain,
    shells,
    onset,
    psi_out,
    energy_out,
    field,
    shell,
    onsets,
    zmid,
    zlow,
    zhigh,
    outer,
    inner,
    firsts,
    seconds,
    binned,
    parts,
    got,
    got_x,
    summed,
    in_sem,
    sent_sem,
    came_sem,
    know,
):
    nx, ny, nz = sizes
    gx, gy, gz = (lax.axis_index(a) for a in ("gx", "gy", "gz"))
    no = jnp.logical_not
    both = jnp.logical_and

    def when(cond, act):
        if cond is None:
            act()
        else:
            pl.when(cond)(act)

    def tell(sem, peer, cond=None):
        when(cond, lambda: pl.semaphore_signal(sem, inc=1, device_id=peer, device_id_type=MESH))

    def total_of(conds):
        return sum(c.astype(jnp.int32) for c in conds)

    def near_to(dy, dz):
        peer = {}
        if dy:
            peer["gy"] = lax.rem(gy + (dy + ny), ny)
        if dz:
            peer["gz"] = lax.rem(gz + (dz + nz), nz)
        return peer

    around = [(dy, dz) for dy in (-1, 0, 1) for dz in (-1, 0, 1) if dy or dz]

    barrier = pltpu.get_barrier_semaphore()
    x_lo, x_hi = gx > 0, gx < nx - 1
    y_lo, y_hi = gy > 0, gy < ny - 1
    z_lo, z_hi = gz > 0, gz < nz - 1
    half = nx // 2
    late, soon = both(x_hi, gx < half), both(x_hi, gx >= half)
    for step in around:
        tell(barrier, near_to(*step))
    for d in range(1, nx):
        tell(barrier, {"gx": gx + d}, gx + d < nx)
    greeted = 8 + gx

    for h in range(2):
        for c in range(CT):
            pltpu.make_async_copy(
                strain.at[c, 8 * h : 8 * h + 8],
                field.at[8 * h + 2 : 8 * h + 10, 2:18, c],
                in_sem.at[h],
            ).start()
    labels = pltpu.make_async_copy(shells, shell, in_sem.at[2])
    starts = pltpu.make_async_copy(onset, onsets, in_sem.at[3])
    labels.start()
    starts.start()

    def zero(cond, ref):
        @pl.when(cond)
        def _():
            ref[...] = jnp.zeros(ref.shape, F32)

    zero(no(x_lo), field.at[0:2, 2:18])
    zero(no(x_hi), field.at[18:20, 2:18])
    zero(no(y_lo), field.at[2:18, 0:2])
    zero(no(y_hi), field.at[2:18, 18:20])
    zero(no(y_lo), zmid.at[0])
    zero(no(y_hi), zmid.at[9])
    zero(no(z_lo), zlow.at[1:9])
    zero(no(z_hi), zhigh.at[1:9])
    zero(no(both(y_lo, z_lo)), zlow.at[0])
    zero(no(both(y_hi, z_lo)), zlow.at[9])
    zero(no(both(y_lo, z_hi)), zhigh.at[0])
    zero(no(both(y_hi, z_hi)), zhigh.at[9])

    lane = lax.broadcasted_iota(jnp.int32, (8, 128), 1)
    sub = lax.broadcasted_iota(jnp.int32, (8, 128), 0)
    slot_of = ((lane + 2) & 127) >> 2
    quarter = lane & 3

    for h in range(2):
        own = field.at[8 * h + 2 : 8 * h + 10, 2:18]
        pltpu.make_async_copy(own, own, in_sem.at[h]).wait()

    packed = [jnp.zeros((8, 128), F32) for _ in range(8)]
    for s in range(32):
        mine = slot_of == s
        for b in range(8):
            row = field[s // 2 + 2, 2 * b + s % 2 + 2]
            moved = pltpu.roll(row, 4 * s, 1) if s else row
            packed[b] = jnp.where(mine, moved, packed[b])
    for b in range(8):
        zmid[b + 1] = packed[b]

    pl.semaphore_wait(barrier, greeted)

    tell(know.at[0], {"gx": gx - 1}, x_lo)
    for step in around:
        tell(know.at[1], near_to(*step))
    for d in range(1, nx):
        tell(know.at[3], {"gx": gx - d}, gx >= d)

    def remote(src, dst, send, recv, peer):
        return pltpu.make_async_remote_copy(
            src_ref=src, dst_ref=dst, send_sem=send, recv_sem=recv, device_id=peer, device_id_type=MESH
        )

    halos = [
        (zmid.at[1:9], zlow.at[1:9], (0, 1), 0),
        (zmid.at[1:9], zhigh.at[1:9], (0, -1), 0),
        (zmid.at[8], zlow.at[0], (1, 1), 1),
        (zmid.at[8], zhigh.at[0], (1, -1), 1),
        (zmid.at[1], zlow.at[9], (-1, 1), 1),
        (zmid.at[1], zhigh.at[9], (-1, -1), 1),
        (zmid.at[8], zmid.at[0], (1, 0), 1),
        (zmid.at[1], zmid.at[9], (-1, 0), 1),
    ]
    def send(halos):
        for src, dst, (dy, dz), i in halos:
            is_there = {(0, 1): z_hi, (0, -1): z_lo, (1, 0): y_hi, (-1, 0): y_lo}
            there = is_there.get((dy, dz))
            if there is None:
                there = both(is_there[dy, 0], is_there[0, dz])
            when(there, remote(src, dst, sent_sem.at[i // 2], came_sem.at[i], near_to(dy, dz)).start)
    y_halos = [
        (field.at[2:18, 16:18], field.at[2:18, 0:2], (1, 0), 2),
        (field.at[2:18, 2:4], field.at[2:18, 18:20], (-1, 0), 2),
    ]
    send(halos)
    send(y_halos)
    y_two, z_two = both(y_lo, y_hi), both(z_lo, z_hi)

    def flush(sem, tiles):
        for y_count in (1, 2):
            for z_count in (1, 2):
                n = tiles(y_count, z_count)
                ref = field.at[0, 0:n] if n <= 20 else field.at[0:4, 0 : n // 4] if n % 4 == 0 else field.at[0:2, 0 : n // 2]
                wait = pltpu.make_async_copy(ref, ref, sem).wait
                when(both(y_two if y_count == 2 else no(y_two), z_two if z_count == 2 else no(z_two)), wait)

    x_down = remote(
        field.at[2:4, 2:18], field.at[18:20, 2:18], sent_sem.at[2], came_sem.at[4], {"gx": gx - 1}
    )
    x_up = remote(
        field.at[16:18, 2:18], field.at[0:2, 2:18], sent_sem.at[3], came_sem.at[5], {"gx": gx + 1}
    )
    when(x_lo, x_down.start)

    labels.wait()
    starts.wait()
    outer[...] = shell[...] >> 5
    inner[...] = shell[...] & 31
    first = jnp.broadcast_to(onsets[pl.ds(gy // 4, 1), :], (8, 128))
    first = pltpu.roll(first, lax.rem(128 - 32 * lax.rem(gy, 4), 128), 1)
    first = jnp.where(lane < 32, first, 0)
    first = first + pltpu.roll(first, 32, 1)
    first = first + pltpu.roll(first, 64, 1)

    signs = jnp.where(sub < 4, 1.0 / 24.0, -1.0 / 24.0).astype(F32)
    minus = -signs

    def shifts(f):
        return (pltpu.roll(f, k, 1) for k in (127, 126, 1, 2))

    def slope(up1, up2, down1, down2):
        d = (up1 - down1) * (8.0 / 144.0) - (up2 - down2) * (1.0 / 144.0)
        return pltpu.roll(d, 4, 0)

    def stars(x, y):
        near = (field[x + 1, y + 2] + field[x + 3, y + 2]) + (field[x + 2, y + 1] + field[x + 2, y + 3])
        far = (field[x, y + 2] + field[x + 4, y + 2]) + (field[x + 2, y] + field[x + 2, y + 4])
        return (16.0 * near - far) * signs

    def along_z(xs, whole):
        for x in xs:
            for y in range(16):
                f = field[x + 2, y + 2]
                up1, up2, down1, down2 = shifts(f)
                firsts[x, y + 2] = slope(up1, up2, down1, down2)
                bend = 16.0 * (up1 + down1) - (up2 + down2)
                value = (bend + 30.0 * f) * minus
                if whole and 2 <= y < 14:
                    value = value + stars(x, y)
                seconds[x, y] = value
        return 0

    lax.fori_loop(0, 3, lambda i, _: along_z([4 * i + 2 + j for j in range(4)], True), 0)
    when(soon, lambda: pl.semaphore_wait(know.at[0], 1))
    when(soon, x_up.start)
    lax.fori_loop(0, 2, lambda i, _: along_z([14 * i, 14 * i + 1], False), 0)

    flush(came_sem.at[0], lambda y, z: 8 * z)

    pl.semaphore_wait(know.at[1], 8)
    for dy, dz in around:
        tell(know.at[2], near_to(2 * dy, 2 * dz))

    when(late, lambda: pl.semaphore_wait(know.at[0], 1))
    when(late, x_up.start)

    even = (slot_of & 1) == 0
    at_end = jnp.logical_or(lane < 2, lane >= 126)
    turns = {}

    def turn(b):
        wrong = jnp.where(quarter >= 2, zlow[b], zhigh[b]) - zmid[b]
        near = jnp.where(
            quarter == 0, pltpu.roll(wrong, 1, 1), jnp.where(quarter == 3, pltpu.roll(wrong, 127, 1), 0.0)
        )
        far = jnp.where(quarter < 2, pltpu.roll(wrong, 2, 1), pltpu.roll(wrong, 126, 1))
        error = far - 8.0 * near
        error = jnp.where(quarter < 2, error, -error)
        turns[b] = (error, pltpu.roll(error, 124, 1), pltpu.roll(error, 4, 1), 16.0 * near - far)

    def mend(b):
        (before, before_up, _, _), (_, up, down, bend), (after, _, after_down, _) = (
            turns[b - 1],
            turns[b],
            turns[b + 1],
        )
        step1 = jnp.where(even, up - before_up, after_down - down)
        mixed = 8.0 * step1 - (after - before)
        fix = bend * minus - pltpu.roll(mixed, 4, 0) * (1.0 / 144.0)
        for s in range(32):
            x, y = s // 2, 2 * b - 2 + s % 2
            end = pltpu.roll(fix, 128 - 4 * s, 1) if s else fix
            seconds[x, y] = seconds[x, y] + jnp.where(at_end, end, 0.0)

    for b in range(1, 9):
        turn(b)
    for b in range(2, 8):
        mend(b)

    step_of = sub & 3
    uz = (lane + gz * 128).astype(F32)
    uz = (uz + 0.5) / (nz * 128) - 0.5
    uz2 = (uz * uz + 0.05) * 0.0625

    def rows(xs, ys, whole=False):
        lefts, rights = [], []
        for x in xs:
            ux = (x + gx * 16).astype(F32)
            ux = (ux + 0.5) / (nx * 16) - 0.5
            ux2 = uz2 + ux * ux * 0.0625
            for y in ys:
                mixed = 8.0 * (firsts[x, y + 3] - firsts[x, y + 1]) - (firsts[x, y + 4] - firsts[x, y])
                value = seconds[x, y] - mixed
                if not whole:
                    value = value + stars(x, y)
                psi_out[x, y] = value
                news = value + jnp.where(step_of >= 1, pltpu.roll(value, 1, 0), 0.0)
                news = news + jnp.where(step_of >= 2, pltpu.roll(news, 2, 0), 0.0)
                power = news * news
                power = power + pltpu.roll(power, 4, 0)
                uy = (gy * 16 + y).astype(F32)
                uy = (uy + 0.5) / (ny * 16) - 0.5
                flux = power * (ux2 + uy * uy * 0.0625)
                high = flux.astype(jnp.bfloat16).astype(F32)
                split = jnp.where(sub < 4, high, flux - high)
                high_label = jnp.broadcast_to(outer[x, pl.ds(y, 1), :], (8, 128))
                low_label = jnp.broadcast_to(inner[x, pl.ds(y, 1), :], (8, 128))
                lefts.append(
                    jnp.concatenate([jnp.where(high_label == k, split, 0.0) for k in range(8)], axis=0)
                )
                rights.append(
                    jnp.concatenate(
                        [jnp.where(low_label == sub + 8 * j, 1.0, 0.0).astype(F32) for j in range(4)], axis=0
                    )
                )
        left = jnp.concatenate(lefts, axis=1)
        right = jnp.concatenate(rights, axis=1)
        return lax.dot_general(left, right, (((1,), (1,)), ((), ())), preferred_element_type=F32)

    total = lax.fori_loop(
        0,
        4,
        lambda i, t: t + rows([3 * i + 2 + j for j in range(3)], range(2, 14), True),
        jnp.zeros((64, 32), F32),
    )
    binned[...] = jnp.zeros((64, 128), F32)
    binned[:, 0:32] = total

    def x_rows():
        when(x_hi, x_down.wait_recv)
        when(x_lo, x_up.wait_recv)
        binned[:, 0:32] += rows((0, 1, 14, 15), range(2, 14))

    x_last = jnp.logical_or(gx == half - 1, gx == half)

    def y_rows():
        flush(came_sem.at[1], lambda y, z: y * (z + 1))
        flush(came_sem.at[2], lambda y, z: 32 * y)

        def y_ends(xs):
            for x in xs:
                for y in (0, 1, 18, 19):
                    up1, up2, down1, down2 = shifts(field[x + 2, y])
                    firsts[x, y] = slope(up1, up2, down1, down2)

        y_ends(range(16))
        for b in (0, 1, 2, 7, 8, 9):
            turn(b)
        for b in (1, 8):
            mend(b)
        binned[:, 0:32] += rows(range(2, 14), (0, 1, 14, 15))

    def in_turn(i, _):
        x_now = (i == 0) != x_last
        when(x_now, x_rows)
        when(no(x_now), y_rows)
        return 0

    lax.fori_loop(0, 2, in_turn, 0)

    binned[:, 0:32] += rows((0, 1, 14, 15), (0, 1, 14, 15))

    pl.semaphore_wait(know.at[2], 8)

    def by_step(x, moves):
        moved = x
        for t in range(1, 4):
            moved = jnp.where(step_of == t, pltpu.roll(x, moves[t], 1), moved)
        return moved

    for k in range(8):
        spread = by_step(binned[8 * k : 8 * k + 8, :], (0, 32, 64, 96))
        parts[k] = jnp.sum(spread, axis=0, keepdims=True)

    offsets = [(dy, dz) for dy in range(ny) for dz in range(nz) if dy or dz]
    offsets.sort(key=lambda o: -(min(o[0], ny - o[0]) + min(o[1], nz - o[1]) / 2))
    for i, (dy, dz) in enumerate(offsets):
        peer = near_to(dy, dz)
        remote(parts.at[peer.get("gy", gy)], got.at[i], sent_sem.at[4], came_sem.at[6], peer).start()

    pltpu.make_async_copy(got, got, came_sem.at[6]).wait()
    sums = [parts[gy]] + [got[i] for i in range(len(offsets))]
    while len(sums) > 1:
        sums = [a + b for a, b in zip(sums[::2], sums[1::2])]
    value = sums[0]

    summed[0] = value
    when(x_hi, lambda: pl.semaphore_wait(know.at[3], nx - 1 - gx))
    for d in range(1, nx):
        copy = remote(summed.at[0], got_x.at[d - 1], sent_sem.at[5], came_sem.at[7], {"gx": gx + d})
        when(gx + d < nx, copy.start)
    for n in range(1, nx):
        when(gx == n, pltpu.make_async_copy(got_x.at[0:n], got_x.at[0:n], came_sem.at[7]).wait)
    for d in range(1, nx):
        value = value + jnp.where(gx >= d, got_x[d - 1], 0.0)

    value = jnp.broadcast_to(value, (8, 128))
    value = jnp.where((lane >> 5) >= first, value, 0.0)
    value = value * (0.25 * 256 / (nx * 16 * ny * 16 * nz * 128))
    steps = [pltpu.roll(value, lax.rem(256 - 32 * t - 4 * gz, 128), 1) for t in range(4)]
    value = steps[0]
    for t in range(1, 4):
        value = value + jnp.where(sub >= t, steps[t], 0.0)
    energy_out[0] = value[0:4, 0:4]

    def left(i, ref):
        pltpu.make_async_copy(ref, ref, sent_sem.at[i]).wait()

    flush(sent_sem.at[0], lambda y, z: 8 * z + y * (z + 1))
    flush(sent_sem.at[1], lambda y, z: 32 * y)
    when(x_lo, x_down.wait_send)
    when(x_hi, x_up.wait_send)
    left(4, got)
    for n in range(1, nx):
        when(gx == nx - 1 - n, lambda n=n: left(5, got_x.at[0:n]))


def write(psi, energy, psi_out, energy_out, sem):
    for c in range(CT):
        pltpu.make_async_copy(psi.at[:, :, c], psi_out.at[c], sem.at[0]).start()
    small = pltpu.make_async_copy(energy, energy_out, sem.at[1])
    small.start()
    pltpu.make_async_copy(psi_out, psi_out, sem.at[0]).wait()
    small.wait()


def solution(mesh):
    sizes = tuple(mesh.shape[a] for a in ("gx", "gy", "gz"))
    vmem = pl.BlockSpec(memory_space=pltpu.VMEM)
    hbm = pl.BlockSpec(memory_space=pltpu.HBM)

    def body(strain, cell_shell_index, onset_step):
        psi, energy = pl.pallas_call(
            lambda *refs: kernel(sizes, *refs),
            out_shape=(pltpu.VMEM((16, 16, 8, 128), F32), pltpu.VMEM((1, 4, 4), F32)),
            in_specs=[hbm] * 3,
            out_specs=(vmem, vmem),
            scratch_shapes=[
                pltpu.VMEM((20, 20, 8, 128), F32),
                pltpu.VMEM((16, 16, 128), jnp.int32),
                pltpu.VMEM((2, 128), jnp.int32),
                pltpu.VMEM((10, 8, 128), F32),
                pltpu.VMEM((10, 8, 128), F32),
                pltpu.VMEM((10, 8, 128), F32),
                pltpu.VMEM((16, 16, 128), jnp.int32),
                pltpu.VMEM((16, 16, 128), jnp.int32),
                pltpu.VMEM((16, 20, 8, 128), F32),
                pltpu.VMEM((16, 16, 8, 128), F32),
                pltpu.VMEM((64, 128), F32),
                pltpu.VMEM((8, 1, 128), F32),
                pltpu.VMEM((63, 1, 128), F32),
                pltpu.VMEM((7, 1, 128), F32),
                pltpu.VMEM((1, 1, 128), F32),
                pltpu.SemaphoreType.DMA((4,)),
                pltpu.SemaphoreType.DMA((6,)),
                pltpu.SemaphoreType.DMA((8,)),
                pltpu.SemaphoreType.REGULAR((4,)),
            ],
            compiler_params=pltpu.CompilerParams(collective_id=0, has_side_effects=True),
        )(strain.reshape(8, 16, 16, 128), cell_shell_index, onset_step.reshape(2, 128))
        psi_four, energy = pl.pallas_call(
            write,
            out_shape=(
                jax.ShapeDtypeStruct((8, 16, 16, 128), F32),
                jax.ShapeDtypeStruct((1, 4, 4), F32),
            ),
            in_specs=[vmem] * 2,
            out_specs=(hbm, hbm),
            scratch_shapes=[pltpu.SemaphoreType.DMA((2,))],
        )(*(pltpu.with_memory_space_constraint(a, pltpu.VMEM) for a in (psi, energy)))
        return psi_four.reshape(strain.shape), energy

    placed = (P(None, None, "gx", "gy", "gz"), P("gx", "gy", "gz"), P())
    return jax.shard_map(
        body,
        mesh=mesh,
        in_specs=placed,
        out_specs=(P(None, None, "gx", "gy", "gz"), P("gx", None, ("gy", "gz"))),
        check_vma=False,
    )
```

time: 24.5 us -> 24 us (0.980)
  Pallas kernels: 23.7 us -> 23.3 us
    pallas_call x1, Pallas kernels: 22.7 us -> 22.3 us  [body(): pl.pallas_call(lambda *refs: kernel(sizes, *refs), out_shape=(pltpu.VMEM(...]
where the time goes in v4:
time: 24 us; the launch traced here: 23.9 us
  Pallas kernels  23.3 us (97%)
  between operations  0.64 us (3%)
    pallas_call x1, Pallas kernels, body(): pl.pallas_call(lambda *refs: kernel(sizes, *refs), out_shape=(pltpu.VMEM(...  22.3 us
    pallas_call x1, Pallas kernels, body(): pl.pallas_call(write, out_shape=(jax.ShapeDtypeStruct((8, 16, 16, 128), F...  0.98 us

profile of v4, /device:TPU:320, one launch (start us, length us, event | category | flops | bytes accessed | tf_op | source)
XLA Modules:
  0.0 23.9 jit_solution(8485312872930898322)
XLA Ops:
  0.6 22.3 %shard_map.50 = (f32[16,16,8,128]{3,2,1,0:T(8,128)S(1)}, f32[1,4,4]{2,1,0:T(4,128)S(1)}) custom-call(f32[8,16,16,128]{3,2,1,0:T(8,128)} %bitcast.3, s32[16,16,128]{2,1,0:T(8,128)} %refs_1_.1, s32[2,128]{1,0:T(2,128)} %bitcast.4), custom_call_target="tpu_custom_call" | custom-call | tf_op jit(solution)/shard_map/pallas_call | solution.py:420
  22.9 1.0 %shard_map.51 = (f32[8,16,16,128]{3,2,1,0:T(8,128)}, f32[1,4,4]{2,1,0:T(4,128)}) custom-call(f32[16,16,8,128]{3,2,1,0:T(8,128)S(1)} %get-tuple-element.6.psi, f32[1,4,4]{2,1,0:T(4,128)S(1)} %get-tuple-element.7.energy), custom_call_target="tpu_custom_call" | custom-call | tf_op jit(solution)/shard_map/pallas_call | solution.py:448

commit v5 on v4

--- a/solution.py
+++ b/solution.py
@@ -70,18 +70,19 @@
     z_lo, z_hi = gz > 0, gz < nz - 1
     half = nx // 2
     late, soon = both(x_hi, gx < half), both(x_hi, gx >= half)
+    tell(barrier, {"gx": gx - 1}, gx > half)
     for step in around:
         tell(barrier, near_to(*step))
     for d in range(1, nx):
         tell(barrier, {"gx": gx + d}, gx + d < nx)
-    greeted = 8 + gx
-
-    for h in range(2):
+    greeted = 8 + gx + total_of((soon,))
+
+    for h in range(4):
         for c in range(CT):
             pltpu.make_async_copy(
-                strain.at[c, 8 * h : 8 * h + 8],
-                field.at[8 * h + 2 : 8 * h + 10, 2:18, c],
-                in_sem.at[h],
+                strain.at[c, 4 * h : 4 * h + 4],
+                field.at[4 * h + 2 : 4 * h + 6, 2:18, c],
+                in_sem.at[h // 2],
             ).start()
     labels = pltpu.make_async_copy(shells, shell, in_sem.at[2])
     starts = pltpu.make_async_copy(onset, onsets, in_sem.at[3])
@@ -115,19 +116,22 @@
         own = field.at[8 * h + 2 : 8 * h + 10, 2:18]
         pltpu.make_async_copy(own, own, in_sem.at[h]).wait()
 
-    packed = [jnp.zeros((8, 128), F32) for _ in range(8)]
-    for s in range(32):
-        mine = slot_of == s
-        for b in range(8):
-            row = field[s // 2 + 2, 2 * b + s % 2 + 2]
-            moved = pltpu.roll(row, 4 * s, 1) if s else row
-            packed[b] = jnp.where(mine, moved, packed[b])
-    for b in range(8):
-        zmid[b + 1] = packed[b]
+    def pack(bs):
+        packed = {b: jnp.zeros((8, 128), F32) for b in bs}
+        for s in range(32):
+            mine = slot_of == s
+            for b in bs:
+                row = field[s // 2 + 2, 2 * b + s % 2 + 2]
+                moved = pltpu.roll(row, 4 * s, 1) if s else row
+                packed[b] = jnp.where(mine, moved, packed[b])
+        for b in bs:
+            zmid[b + 1] = packed[b]
+
+    pack((0, 7))
 
     pl.semaphore_wait(barrier, greeted)
 
-    tell(know.at[0], {"gx": gx - 1}, x_lo)
+    tell(know.at[0], {"gx": gx - 1}, both(x_lo, gx <= half))
     for step in around:
         tell(know.at[1], near_to(*step))
     for d in range(1, nx):
@@ -155,11 +159,12 @@
             if there is None:
                 there = both(is_there[dy, 0], is_there[0, dz])
             when(there, remote(src, dst, sent_sem.at[i // 2], came_sem.at[i], near_to(dy, dz)).start)
-    y_halos = [
-        (field.at[2:18, 16:18], field.at[2:18, 0:2], (1, 0), 2),
-        (field.at[2:18, 2:4], field.at[2:18, 18:20], (-1, 0), 2),
-    ]
-    send(halos)
+    y_halos = []
+    for h in range(2):
+        mine = pl.ds(8 * h + 2, 8)
+        y_halos.append((field.at[mine, 16:18], field.at[mine, 0:2], (1, 0), 2 + h))
+        y_halos.append((field.at[mine, 2:4], field.at[mine, 18:20], (-1, 0), 2 + h))
+    send(halos[2:])
     send(y_halos)
     y_two, z_two = both(y_lo, y_hi), both(z_lo, z_hi)
 
@@ -178,6 +183,9 @@
         field.at[16:18, 2:18], field.at[0:2, 2:18], sent_sem.at[3], came_sem.at[5], {"gx": gx + 1}
     )
     when(x_lo, x_down.start)
+    when(soon, x_up.start)
+    pack(range(1, 7))
+    send(halos[:2])
 
     labels.wait()
     starts.wait()
@@ -218,8 +226,6 @@
         return 0
 
     lax.fori_loop(0, 3, lambda i, _: along_z([4 * i + 2 + j for j in range(4)], True), 0)
-    when(soon, lambda: pl.semaphore_wait(know.at[0], 1))
-    when(soon, x_up.start)
     lax.fori_loop(0, 2, lambda i, _: along_z([14 * i, 14 * i + 1], False), 0)
 
     flush(came_sem.at[0], lambda y, z: 8 * z)
@@ -322,7 +328,7 @@
 
     def y_rows():
         flush(came_sem.at[1], lambda y, z: y * (z + 1))
-        flush(came_sem.at[2], lambda y, z: 32 * y)
+        flush(came_sem.at[2], lambda y, z: 16 * y)
 
         def y_ends(xs):
             for x in xs:
@@ -330,12 +336,15 @@
                     up1, up2, down1, down2 = shifts(field[x + 2, y])
                     firsts[x, y] = slope(up1, up2, down1, down2)
 
-        y_ends(range(16))
+        y_ends(range(8))
         for b in (0, 1, 2, 7, 8, 9):
             turn(b)
         for b in (1, 8):
             mend(b)
-        binned[:, 0:32] += rows(range(2, 14), (0, 1, 14, 15))
+        binned[:, 0:32] += rows(range(2, 8), (0, 1, 14, 15))
+        flush(came_sem.at[3], lambda y, z: 16 * y)
+        y_ends(range(8, 16))
+        binned[:, 0:32] += rows(range(8, 14), (0, 1, 14, 15))
 
     def in_turn(i, _):
         x_now = (i == 0) != x_last
@@ -404,7 +413,9 @@
 
 def write(psi, energy, psi_out, energy_out, sem):
     for c in range(CT):
-        pltpu.make_async_copy(psi.at[:, :, c], psi_out.at[c], sem.at[0]).start()
+        for h in range(4):
+            mine = pl.ds(4 * h, 4)
+            pltpu.make_async_copy(psi.at[mine, :, c], psi_out.at[c, mine], sem.at[0]).start()
     small = pltpu.make_async_copy(energy, energy_out, sem.at[1])
     small.start()
     pltpu.make_async_copy(psi_out, psi_out, sem.at[0]).wait()

time: 24 us -> 23.8 us (level)
  Pallas kernels: 23.3 us -> 23 us
where the time goes in v5:
time: 23.8 us; the launch traced here: 23.7 us
  Pallas kernels  23 us (97%)
  between operations  0.64 us (3%)
    pallas_call x1, Pallas kernels, body(): pl.pallas_call(lambda *refs: kernel(sizes, *refs), out_shape=(pltpu.VMEM(...  22.1 us
    pallas_call x1, Pallas kernels, body(): pl.pallas_call(write, out_shape=(jax.ShapeDtypeStruct((8, 16, 16, 128), F...  0.96 us

profile of v5, /device:TPU:320, one launch (start us, length us, event | category | flops | bytes accessed | tf_op | source)
XLA Modules:
  0.0 23.7 jit_solution(15838388569988546452)
XLA Ops:
  0.6 22.1 %shard_map.50 = (f32[16,16,8,128]{3,2,1,0:T(8,128)S(1)}, f32[1,4,4]{2,1,0:T(4,128)S(1)}) custom-call(f32[8,16,16,128]{3,2,1,0:T(8,128)} %bitcast.3, s32[16,16,128]{2,1,0:T(8,128)} %refs_1_.1, s32[2,128]{1,0:T(2,128)} %bitcast.4), custom_call_target="tpu_custom_call" | custom-call | tf_op jit(solution)/shard_map/pallas_call | solution.py:431
  22.7 1.0 %shard_map.51 = (f32[8,16,16,128]{3,2,1,0:T(8,128)}, f32[1,4,4]{2,1,0:T(4,128)}) custom-call(f32[16,16,8,128]{3,2,1,0:T(8,128)S(1)} %get-tuple-element.6.psi, f32[1,4,4]{2,1,0:T(4,128)S(1)} %get-tuple-element.7.energy), custom_call_target="tpu_custom_call" | custom-call | tf_op jit(solution)/shard_map/pallas_call | solution.py:459

commit v6 on v5

--- a/solution.py
+++ b/solution.py
@@ -228,14 +228,14 @@
     lax.fori_loop(0, 3, lambda i, _: along_z([4 * i + 2 + j for j in range(4)], True), 0)
     lax.fori_loop(0, 2, lambda i, _: along_z([14 * i, 14 * i + 1], False), 0)
 
+    when(late, lambda: pl.semaphore_wait(know.at[0], 1))
+    when(late, x_up.start)
+
     flush(came_sem.at[0], lambda y, z: 8 * z)
 
     pl.semaphore_wait(know.at[1], 8)
     for dy, dz in around:
         tell(know.at[2], near_to(2 * dy, 2 * dz))
-
-    when(late, lambda: pl.semaphore_wait(know.at[0], 1))
-    when(late, x_up.start)
 
     even = (slot_of & 1) == 0
     at_end = jnp.logical_or(lane < 2, lane >= 126)

time: 23.8 us -> 23.7 us (level)
  no operation moved by 1% of the time
where the time goes in v6:
time: 23.7 us; the launch traced here: 23.6 us
  Pallas kernels  22.9 us (97%)
  between operations  0.64 us (3%)
    pallas_call x1, Pallas kernels, body(): pl.pallas_call(lambda *refs: kernel(sizes, *refs), out_shape=(pltpu.VMEM(...  22 us
    pallas_call x1, Pallas kernels, body(): pl.pallas_call(write, out_shape=(jax.ShapeDtypeStruct((8, 16, 16, 128), F...  0.96 us

profile of v6, /device:TPU:320, one launch (start us, length us, event | category | flops | bytes accessed | tf_op | source)
XLA Modules:
  0.0 23.6 jit_solution(13526313831572248644)
XLA Ops:
  0.6 22.0 %shard_map.50 = (f32[16,16,8,128]{3,2,1,0:T(8,128)S(1)}, f32[1,4,4]{2,1,0:T(4,128)S(1)}) custom-call(f32[8,16,16,128]{3,2,1,0:T(8,128)} %bitcast.3, s32[16,16,128]{2,1,0:T(8,128)} %refs_1_.1, s32[2,128]{1,0:T(2,128)} %bitcast.4), custom_call_target="tpu_custom_call" | custom-call | tf_op jit(solution)/shard_map/pallas_call | solution.py:431
  22.6 1.0 %shard_map.51 = (f32[8,16,16,128]{3,2,1,0:T(8,128)}, f32[1,4,4]{2,1,0:T(4,128)}) custom-call(f32[16,16,8,128]{3,2,1,0:T(8,128)S(1)} %get-tuple-element.6.psi, f32[1,4,4]{2,1,0:T(4,128)S(1)} %get-tuple-element.7.energy), custom_call_target="tpu_custom_call" | custom-call | tf_op jit(solution)/shard_map/pallas_call | solution.py:459

commit v7 on v6

--- a/solution.py
+++ b/solution.py
@@ -312,8 +312,8 @@
 
     total = lax.fori_loop(
         0,
-        4,
-        lambda i, t: t + rows([3 * i + 2 + j for j in range(3)], range(2, 14), True),
+        2,
+        lambda i, t: t + rows([6 * i + 2 + j for j in range(6)], range(2, 14), True),
         jnp.zeros((64, 32), F32),
     )
     binned[...] = jnp.zeros((64, 128), F32)
@@ -382,7 +382,7 @@
 
     summed[0] = value
     when(x_hi, lambda: pl.semaphore_wait(know.at[3], nx - 1 - gx))
-    for d in range(1, nx):
+    for d in reversed(range(1, nx)):
         copy = remote(summed.at[0], got_x.at[d - 1], sent_sem.at[5], came_sem.at[7], {"gx": gx + d})
         when(gx + d < nx, copy.start)
     for n in range(1, nx):

time: 23.7 us -> 23.7 us (level)
  no operation moved by 1% of the time
where the time goes in v7:
time: 23.7 us; the launch traced here: 23.6 us
  Pallas kernels  22.9 us (97%)
  between operations  0.64 us (3%)
    pallas_call x1, Pallas kernels, body(): pl.pallas_call(lambda *refs: kernel(sizes, *refs), out_shape=(pltpu.VMEM(...  22 us
    pallas_call x1, Pallas kernels, body(): pl.pallas_call(write, out_shape=(jax.ShapeDtypeStruct((8, 16, 16, 128), F...  0.96 us

profile of v7, /device:TPU:320, one launch (start us, length us, event | category | flops | bytes accessed | tf_op | source)
XLA Modules:
  0.0 23.6 jit_solution(12648897318697136918)
XLA Ops:
  0.6 22.0 %shard_map.50 = (f32[16,16,8,128]{3,2,1,0:T(8,128)S(1)}, f32[1,4,4]{2,1,0:T(4,128)S(1)}) custom-call(f32[8,16,16,128]{3,2,1,0:T(8,128)} %bitcast.3, s32[16,16,128]{2,1,0:T(8,128)} %refs_1_.1, s32[2,128]{1,0:T(2,128)} %bitcast.4), custom_call_target="tpu_custom_call" | custom-call | tf_op jit(solution)/shard_map/pallas_call | solution.py:431
  22.6 1.0 %shard_map.51 = (f32[8,16,16,128]{3,2,1,0:T(8,128)}, f32[1,4,4]{2,1,0:T(4,128)}) custom-call(f32[16,16,8,128]{3,2,1,0:T(8,128)S(1)} %get-tuple-element.6.psi, f32[1,4,4]{2,1,0:T(4,128)S(1)} %get-tuple-element.7.energy), custom_call_target="tpu_custom_call" | custom-call | tf_op jit(solution)/shard_map/pallas_call | solution.py:459
